TPU v7x, 256 devices: a whole 4x4x8 slice. The times are simulated.
256 devices in a mesh: dp: 4 (over x), expert: 32 (over y, z), tensor: 2 (over core).
Axes of the slice: x: 4, y: 4, z: 8, core: 2. Of those that a mesh axis runs over, the one named last changes fastest.
Arguments:
- tokens: bfloat16 [16384, 2560], P(('dp', 'expert')), may hold values from -6 to 6
- norm_gain: float32 [2560], replicated, may hold values from 0.5 to 1.5
- expert_ids: int32 [16384, 6], P(('dp', 'expert')), may hold values from 0 to 31, all different within a row; in each aligned block of 128 rows (0 to 127, 128 to 255, ...) at most 48 rows name the same one
- route_weights: int32 [16384, 6], P(('dp', 'expert')), may hold values from 1 to 64
- w_gate: bfloat16 [32, 2560, 768], P('expert', None, 'tensor'), may hold values from -0.125 to 0.125
- w_up: bfloat16 [32, 2560, 768], P('expert', None, 'tensor'), may hold values from -0.125 to 0.125
- w_down: bfloat16 [32, 768, 2560], P('expert', 'tensor'), may hold values from -0.21875 to 0.21875
- shared_gate: bfloat16 [2560, 2048], P(None, ('dp', 'tensor')), may hold values from -0.125 to 0.125
- shared_up: bfloat16 [2560, 2048], P(None, ('dp', 'tensor')), may hold values from -0.125 to 0.125
- shared_down: bfloat16 [2048, 2560], P(('dp', 'tensor')), may hold values from -0.125 to 0.125
Outputs:
- mixed: bfloat16 [16384, 2560], P(('dp', 'expert'), 'tensor')
Inputs may be any that keep to these rules, and one draw needn't show every extreme that they name: `expert_ids`: each row names 6 different experts. In each aligned block of 128 rows (the rows of one index of dp+expert) no expert is named by more than 48 rows, a bound that some blocks reach.
All inputs are finite; a program needn't handle non-finite values.
Results may differ from a plain program's by a relative error of at most 0.011.
Values may be sent and summed in bfloat16 or wider, within the bound.
A program may use at most 128 MiB of HBM per device.

v0:
```python
import jax
import jax.numpy as jnp
from jax import lax
from jax.sharding import PartitionSpec as P

D = 2560
EXPERTS = 32
TOP = 6
CAP = 48


EPSILON = 1e-06


def normalize(tokens, norm_gain):
    values = tokens.astype(jnp.float32)
    inverse = lax.rsqrt(jnp.mean(values * values, axis=1, keepdims=True) + EPSILON)
    return (values * inverse * norm_gain[None, :]).astype(jnp.bfloat16)


def slot_positions(expert_ids):
    flat_ids = expert_ids.reshape(-1)
    onehot = (flat_ids[:, None] == jnp.arange(EXPERTS, dtype=jnp.int32)[None, :]).astype(jnp.int32)
    earlier = jnp.cumsum(onehot, axis=0) - onehot
    return flat_ids * CAP + jnp.sum(earlier * onehot, axis=1)


def on_device(
    tokens,
    norm_gain,
    expert_ids,
    route_weights,
    w_gate,
    w_up,
    w_down,
    shared_gate,
    shared_up,
    shared_down,
):
    normed = normalize(tokens, norm_gain)
    tok_rows = normed.shape[0]
    tensor_count = lax.axis_size("tensor")
    half_width = D // tensor_count
    tensor_rank = lax.axis_index("tensor")
    owners = lax.axis_size("expert")
    exp_local = w_gate.shape[0]
    position = slot_positions(expert_ids)
    pair_count = position.shape[0]
    pair_token = jnp.arange(pair_count, dtype=jnp.int32) // TOP
    filler = jnp.full((EXPERTS * CAP,), -1, jnp.int32).at[position].set(pair_token)
    filled = filler >= 0
    safe_rows = jnp.maximum(filler, 0)
    source_rows = lax.dynamic_slice_in_dim(normed, tensor_rank * half_width, half_width, 1)
    outgoing = jnp.where(filled[:, None], source_rows[safe_rows], jnp.zeros((), jnp.bfloat16))
    outgoing = outgoing.reshape(EXPERTS, CAP, source_rows.shape[1])
    arrived = lax.all_to_all(outgoing, "expert", split_axis=0, concat_axis=0, tiled=True)
    arrived = lax.all_gather(arrived, "tensor", axis=2, tiled=True)
    slot_count = arrived.shape[1]
    grouped = arrived.reshape(owners, exp_local, slot_count, D)
    gate_value = jnp.einsum("jecd,edf->jecf", grouped, w_gate, preferred_element_type=jnp.float32)
    up_value = jnp.einsum("jecd,edf->jecf", grouped, w_up, preferred_element_type=jnp.float32)
    hidden = (jax.nn.silu(gate_value) * up_value).astype(jnp.bfloat16)
    partial_out = jnp.einsum("jecf,efd->jecd", hidden, w_down, preferred_element_type=jnp.float32)
    summed = lax.psum_scatter(
        partial_out.astype(jnp.bfloat16), "tensor", scatter_dimension=3, tiled=True
    )
    summed = summed.reshape(owners * exp_local, slot_count, half_width)
    result_rows = lax.all_to_all(summed, "expert", split_axis=0, concat_axis=0, tiled=True)
    piece_rows = lax.all_gather(normed, "dp", axis=0, tiled=True)
    gate_value = jnp.dot(piece_rows, shared_gate, preferred_element_type=jnp.float32)
    up_value = jnp.dot(piece_rows, shared_up, preferred_element_type=jnp.float32)
    shared_hidden = (jax.nn.silu(gate_value) * up_value).astype(jnp.bfloat16)
    start_row = jnp.int32(0)
    pieces = []
    for offset in range(tok_rows * lax.axis_size(("dp", "tensor")) // tok_rows):
        block_index = start_row // tok_rows + offset
        group_index = block_index // tensor_count
        column_index = block_index % tensor_count
        hidden_block = lax.dynamic_slice_in_dim(shared_hidden, group_index * tok_rows, tok_rows, 0)
        down_block = lax.dynamic_slice_in_dim(shared_down, column_index * half_width, half_width, 1)
        pieces.append(jnp.dot(hidden_block, down_block, preferred_element_type=jnp.float32))
    shared_part = lax.psum_scatter(
        jnp.concatenate(pieces, axis=0).astype(jnp.bfloat16),
        ("dp", "tensor"),
        scatter_dimension=0,
        tiled=True,
    ).astype(jnp.float32)
    table = result_rows.reshape(EXPERTS * CAP, half_width)
    picked = table[position].reshape(tok_rows, TOP, half_width).astype(jnp.float32)
    scales = route_weights.astype(jnp.float32) / 64.0
    routed = jnp.sum(scales[:, :, None] * picked, axis=1)
    return (shared_part + routed).astype(jnp.bfloat16)


def solution(mesh):
    placed = (
        P(("dp", "expert"), None),
        P(),
        P(("dp", "expert"), None),
        P(("dp", "expert"), None),
        P("expert", None, "tensor"),
        P("expert", None, "tensor"),
        P("expert", "tensor", None),
        P(None, ("dp", "tensor")),
        P(None, ("dp", "tensor")),
        P(("dp", "tensor"), None),
    )
    return jax.shard_map(
        on_device,
        mesh=mesh,
        in_specs=placed,
        out_specs=P(("dp", "expert"), "tensor"),
        check_vma=False,
    )
```

profile of v0, /device:TPU:2, one launch (start us, length us, event | category | flops | bytes accessed | tf_op | source)
XLA Modules:
  0.0 321.8 jit_solution(4597402215661047442)
XLA Ops:
  7.4 0.9 copy.14
  8.6 0.7 broadcast_multiply_fusion
  9.3 1.7 reduce-window.6
  11.0 0.3 slice_reduce_fusion
  11.7 3.4 %scatter_custom_fusion = s32[1536]{0:T(1024)S(1)} fusion(s32[768]{0:T(1024)S(1)} %fusion.53, s32[768]{0:T(1024)S(1)} %add_select_fusion, s32[]{:T(128)} %constant.415.clone.1), kind=kCustom, calls=%fused_computation.79 | custom fusion | bytes 6148 | tf_op jit(solution)/shard_map/scatter | solution.py:50
  15.2 1.3 fusion.22
  16.6 1.3 fusion.24
  17.9 6.0 %gather_fusion = bf16[1536,1280]{1,0:T(8,128)(2,1)} fusion(bf16[128,1280]{1,0:T(8,128)(2,1)S(1)} %constant_dynamic-slice_fusion, s32[2048]{0:T(1024)S(1)} %pad_clamp_fusion), kind=kCustom, calls=%fused_computation | custom fusion | bytes 7870464 | tf_op jit(solution)/shard_map/gather | solution.py:54
  24.0 2.4 broadcast_select_fusion
  26.3 101.1 %all_to_all.10 = bf16[32,48,1280]{2,1,0:T(8,128)(2,1)} all-to-all(bf16[32,48,1280]{2,1,0:T(8,128)(2,1)S(1)} %broadcast_select_fusion), channel_id=1, replica_groups=mesh['dp'=4,'expert'=32,'tensor'=2] {'expert'}, dimensions={0} | all-to-all | bytes 7864320 | tf_op jit(solution)/shard_map/all_to_all | solution.py:56
  127.5 21.8 %all-gather.5.cloned.1.call-done = bf16[32,48,2560]{2,1,0:T(8,128)(2,1)} async-done(((bf16[32,48,1280]{2,1,0:T(8,128)(2,1)}), bf16[32,48,2560]{2,1,0:T(8,128)(2,1)}) %all-gather.5.cloned.1.call-update) | async-done | bytes 7864336 | tf_op jit(solution)/shard_map/all_gather | solution.py:57
  149.3 9.4 %fusion.13 = f32[32,48,384]{2,1,0:T(8,128)} fusion(bf16[32,48,2560]{2,1,0:T(8,128)(2,1)} %all-gather.5.cloned.1.call-done, bf16[1,2560,384]{2,1,0:T(8,128)(2,1)} %param.15), kind=kOutput, calls=%fused_computation.30 | convolution fusion | flops 3019898880 | bytes 12189696 | tf_op jit(solution)/shard_map/jecd,edf->jecf/dot_general | solution.py:61
  158.7 13.5 %convert_bitcast_fusion = bf16[32,1,48,2560]{3,2,0,1:T(8,128)(2,1)} fusion(bf16[1,384,2560]{2,1,0:T(8,128)(2,1)S(1)} %copy-done, f32[32,48,384]{2,1,0:T(8,128)} %fusion.13, bf16[32,48,2560]{2,1,0:T(8,128)(2,1)} %all-gather.5.cloned.1.call-done, bf16[1,2560,384]{2,1,0:T(8,128)(2,1)} %param.14), kind=kOutput, calls=%fused_computation.3 | convolution fusion | flops 6047268864 | bytes 22020096 | tf_op jit(solution)/shard_map/jecf,efd->jecd/dot_general | solution.py:63
  172.3 0.5 all-gather.3.cloned.1.call-update
  172.9 21.6 %reduce-scatter.5.cloned.1.call-done = bf16[32,1,48,1280]{3,2,0,1:T(8,128)(2,1)} async-done(((bf16[32,1,48,2560]{3,2,0,1:T(8,128)(2,1)}), bf16[32,1,48,1280]{3,2,0,1:T(8,128)(2,1)}) %reduce-scatter.5.cloned.1.call-update) | async-done | bytes 3932176 | tf_op jit(solution)/shard_map/reduce_scatter | solution.py:64
  194.4 10.0 %all-to-all-start.1 = ((bf16[32,48,1280]{2,1,0:T(8,128)(2,1)}), bf16[32,48,1280]{2,1,0:T(8,128)(2,1)}, u32[]{:S(2)}, u32[]{:S(2)}) async-start(bf16[32,48,1280]{2,1,0:T(8,128)(2,1)} %bitcast.91), calls=%async_computation.3 | async-start | bytes 7864320 | tf_op jit(solution)/shard_map/all_to_all | solution.py:68
  204.7 7.9 %all-gather.3.cloned.1.call-done = bf16[512,2560]{1,0:T(8,128)(2,1)} async-done(((bf16[128,2560]{1,0:T(8,128)(2,1)}), bf16[512,2560]{1,0:T(8,128)(2,1)}) %all-gather.3.cloned.1.call-update) | async-done | bytes 2621456 | tf_op jit(solution)/shard_map/all_gather | solution.py:69
  212.6 3.1 fusion.55
  215.7 2.3 fusion.25
  218.0 1.0 fusion.7
  219.0 1.0 fusion.6
  219.9 1.0 fusion.5
  220.9 1.0 fusion.4
  221.9 1.0 fusion.3
  222.9 1.0 fusion.2
  223.9 1.0 fusion.1
  224.9 1.0 fusion
  226.0 70.2 %all-to-all-done.1 = bf16[32,48,1280]{2,1,0:T(8,128)(2,1)} async-done(((bf16[32,48,1280]{2,1,0:T(8,128)(2,1)}), bf16[32,48,1280]{2,1,0:T(8,128)(2,1)}, u32[]{:S(2)}, u32[]{:S(2)}) %all-to-all-start.1) | async-done | bytes 3932192 | tf_op jit(solution)/shard_map/all_to_all | solution.py:68
  296.2 7.8 %gather_fusion.1 = bf16[768,1280]{1,0:T(8,128)(2,1)} fusion(bf16[1536,1280]{1,0:T(8,128)(2,1)} %bitcast.21, s32[1024]{0:T(1024)S(1)} %pad_clamp_fusion.1), kind=kCustom, calls=%fused_computation.1 | custom fusion | bytes 3935232 | tf_op jit(solution)/shard_map/gather | solution.py:89
  304.0 4.5 %reshape.101 = f32[128,6,1280]{2,1,0:T(8,128)} reshape(bf16[768,1280]{1,0:T(8,128)(2,1)} %gather_fusion.1) | data formatting | bytes 5898240 | tf_op jit(solution)/shard_map/convert_element_type | solution.py:89
  308.5 4.1 %multiply_reduce_fusion = f32[128,1280]{1,0:T(8,128)S(1)} fusion(f32[128,6,1280]{2,1,0:T(8,128)} %reshape.101, f32[128,6]{1,0:T(8,128)S(1)} %copy.12), kind=kLoop, calls=%fused_computation.4 | loop fusion | flops 1802240 | bytes 4590592 | tf_op jit(solution)/shard_map/reduce_sum | solution.py:91
  312.7 1.8 add_convert_fusion
  (36 shorter events, 1.4 us)
Async XLA Ops:
  7.4 151.4 %copy-start = (bf16[1,384,2560]{2,1,0:T(8,128)(2,1)S(1)}, bf16[1,384,2560]{2,1,0:T(8,128)(2,1)}, u32[]{:S(2)}) copy-start(bf16[1,384,2560]{2,1,0:T(8,128)(2,1)} %param.16) | copy-start | bytes 5898244
  7.4 141.9 %all-gather.5.cloned.1.call-start = ((), (), s32[]{:S(2)}) async-start(), calls=%async_computation.6 | async-start | bytes 11796480 | tf_op jit(solution)/shard_map/all_gather | solution.py:57
  17.9 6.1 %copy-start.1 = (bf16[128,2560]{1,0:T(8,128)(2,1)}, bf16[128,2560]{1,0:T(8,128)(2,1)S(1)}, u32[]{:S(2)}) copy-start(bf16[128,2560]{1,0:T(8,128)(2,1)S(1)} %fusion.24) | copy-start | bytes 1966084
  127.5 67.0 %reduce-scatter.5.cloned.1.call-start = ((), (), s32[]{:S(2)}) async-start(), calls=%async_computation.7 | async-start | bytes 11796480 | tf_op jit(solution)/shard_map/reduce_scatter | solution.py:64
  172.3 40.3 %all-gather.3.cloned.1.call-start = ((), (), s32[]{:S(2)}) async-start(), calls=%async_computation.4 | async-start | bytes 3276800 | tf_op jit(solution)/shard_map/all_gather | solution.py:69
  194.4 101.8 %all-to-all-start.1 = ((bf16[32,48,1280]{2,1,0:T(8,128)(2,1)}), bf16[32,48,1280]{2,1,0:T(8,128)(2,1)}, u32[]{:S(2)}, u32[]{:S(2)}) async-start(bf16[32,48,1280]{2,1,0:T(8,128)(2,1)} %bitcast.91), calls=%async_computation.3 | async-start | bytes 7864320 | tf_op jit(solution)/shard_map/all_to_all | solution.py:68
  204.4 108.2 %reduce-scatter.3.cloned.1.call-start = ((), (), s32[]{:S(2)}) async-start(), calls=%async_computation.5 | async-start | bytes 2949120 | tf_op jit(solution)/shard_map/reduce_scatter | solution.py:82
  212.6 3.1 copy-start.3
  215.7 2.3 copy-start.4
  223.9 2.0 copy-start.2
Sparse Core Ops, SparseCore 0:
  127.6 21.6 all-gather.4
  172.4 21.9 reduce-scatter.4
Sparse Core Ops, SparseCore 1:
  174.6 37.9 all-gather.2
  225.9 35.7 reduce-scatter.2
where the time goes:
time: 322 us
  waiting for transfers between devices  122 us (38%)
  blocking collectives  101 us (31%)
  matrix products  36.2 us (11%)
  local copies, waits for them, and re-layouts  23.7 us (7%)
  between operations  15.1 us (5%)
  other arithmetic  13.5 us (4%)
  starting transfers between devices  10.3 us (3%)
    all_to_all x1, blocking collectives, on_device(): lax.all_to_all(outgoing, 'expert', split_axis=0, concat_axis=0, tiled=True)  101 us
    all_to_all x1, waiting for transfers between devices, on_device(): lax.all_to_all(summed, 'expert', split_axis=0, concat_axis=0, tiled=True)  70.2 us
    all_gather x1, waiting for transfers between devices, on_device(): arrived = lax.all_gather(arrived, 'tensor', axis=2, tiled=True)  21.8 us
    reduce_scatter x1, waiting for transfers between devices, on_device(): lax.psum_scatter(partial_out.astype(jnp.bfloat16), 'tensor', scatter_dime...  21.6 us
    dot_general x1, matrix products, on_device(): jnp.einsum('jecf,efd->jecd', hidden, w_down, preferred_element_type=jnp.f...  13.5 us
    all_to_all x1, starting transfers between devices, on_device(): lax.all_to_all(summed, 'expert', split_axis=0, concat_axis=0, tiled=True)  9.96 us
    dot_general x1, matrix products, on_device(): jnp.einsum('jecd,edf->jecf', grouped, w_up, preferred_element_type=jnp.fl...  9.41 us
    all_gather x1, waiting for transfers between devices, on_device(): piece_rows = lax.all_gather(normed, 'dp', axis=0, tiled=True)  7.91 us
  transfers between devices with their start and end apart: 5, of which 4 were waited for; matrix products, arithmetic and copies ran while one was open for 9% of the time, Pallas kernels for 0%

commit v1 on v0

v1 whole, which is shorter than its diff:
```python
import jax
import jax.numpy as jnp
from jax import lax
from jax.experimental import pallas as pl
from jax.experimental.pallas import tpu as pltpu
from jax.sharding import PartitionSpec as P

D = 2560
HALF = D // 2
QUARTER = HALF // 2
FF2 = 384
FF = 768
SF = 256
EXPERTS = 32
TOP = 6
TOK = 128
CAP = 48
YN = 4
ZN = 8
XN = 4
ROWS = YN * CAP
EPSILON = 1e-06
MESH = pl.DeviceIdType.MESH
BF16 = jnp.bfloat16
F32 = jnp.float32


def owner(d):
    return 0 if d < ZN // 2 else 1


def chunk_of(d):
    return d if d < ZN // 2 else ZN - 1 - d


def kernel(
    tokens, gain, ids, weights, wg_in, wu_in, wd_in, sg_in, su_in, sd_in,
    out,
    t_buf, g_buf, code, d_buf, r_buf, h_buf, o_buf, q_buf,
    plus_in, minus_in, plus_out, minus_out, sh_buf, s_in,
    wg, wu, wd, sgu, sd,
    load_sem, wsend_sem, wrecv_sem,
    zsend_sem, zrecv_sem, csend_sem, crecv_sem,
    ysend_sem, yrecv_sem, ysend0_sem, yrecv0_sem,
    bsend_sem, brecv_sem, bsend0_sem, brecv0_sem,
    rsend_sem, rrecv_sem,
    xsend_sem, xrecv_sem, ssend_sem, srecv_sem,
):
    x = lax.axis_index("dp")
    e = lax.axis_index("expert")
    r = lax.axis_index("tensor")
    y = e // ZN
    z = e % ZN
    half = pl.multiple_of(r * HALF, 128)
    other = pl.multiple_of((1 - r) * HALF, 128)

    def at(dx=0, dy=0, dz=0, core=None):
        return (
            (x + dx + XN) % XN,
            ((y + dy + YN) % YN) * ZN + (z + dz + ZN) % ZN,
            r if core is None else core,
        )

    partner = at(core=1 - r)

    def remote(src, dst, send, recv, device):
        return pltpu.make_async_remote_copy(
            src_ref=src, dst_ref=dst, send_sem=send, recv_sem=recv,
            device_id=device, device_id_type=MESH,
        )

    def await_bytes(ref, sem):
        pltpu.make_async_copy(ref, ref, sem).wait()

    barrier = pltpu.get_barrier_semaphore()
    peers = [partner, at(dz=1), at(dz=-1)]
    for k in range(1, YN):
        peers += [at(dy=k), at(dy=k, core=1 - r)]
    for k in range(1, XN):
        peers += [at(dx=k), at(dx=k, core=1 - r)]
    for peer in peers:
        pl.semaphore_signal(barrier, inc=1, device_id=peer, device_id_type=MESH)

    loads = [
        (wg_in.at[0], wg.at[:, pl.ds(0, FF2)]),
        (wu_in.at[0], wu.at[:, pl.ds(0, FF2)]),
        (wd_in.at[0], wd.at[pl.ds(0, FF2), :]),
        (sg_in, sgu.at[:, pl.ds(0, SF)]),
        (su_in, sgu.at[:, pl.ds(SF, SF)]),
        (sd_in, sd),
    ]
    for i, (src, dst) in enumerate(loads):
        pltpu.make_async_copy(src, dst, load_sem.at[i]).start()

    def norm_step(i, carry):
        rows = pl.ds(pl.multiple_of(i * 16, 16), 16)
        values = tokens[rows, :].astype(F32)
        inverse = lax.rsqrt(jnp.mean(values * values, axis=1, keepdims=True) + EPSILON)
        normed = values * inverse * gain[...]
        t_buf[0, rows, :] = normed.astype(BF16)
        g_buf[0, rows, :] = jnp.where(r == 0, normed[:, :HALF], normed[:, HALF:]).astype(BF16)
        return carry

    lax.fori_loop(0, TOK // 16, norm_step, 0)

    lane = lax.broadcasted_iota(jnp.int32, (TOK, 128), 1)
    row = lax.broadcasted_iota(jnp.int32, (TOK, 128), 0)
    named = jnp.zeros((TOK, 128), F32)
    weight = jnp.zeros((TOK, 128), F32)
    for k in range(TOP):
        match = ids[:, k : k + 1] == lane
        named = jnp.where(match, 1.0, named)
        weight = jnp.where(match, weights[:, k : k + 1].astype(F32), weight)
    earlier = jnp.where(lane < row, 1.0, 0.0).astype(BF16)
    rank = jnp.dot(earlier, named.astype(BF16), preferred_element_type=F32)
    packed = jnp.where(named > 0.5, weight * 64.0 + rank, -1.0)
    code[0] = packed.T[:EXPERTS, :]

    pl.semaphore_wait(barrier, len(peers))

    def z_copies(way, k):
        if way == 0:
            here, there, to = k - 1, k, at(dz=-1)
        else:
            here, there, to = (ZN - (k - 1)) % ZN, ZN - k, at(dz=1)
        if k == ZN // 2:
            cols = pl.ds(way * QUARTER, QUARTER)
            src, dst = g_buf.at[here, :, cols], g_buf.at[there, :, cols]
        else:
            src, dst = g_buf.at[here], g_buf.at[there]
        copies = [remote(src, dst, zsend_sem.at[way, k - 1], zrecv_sem.at[way, k - 1], to)]
        if k < ZN // 2 or way == 0:
            copies.append(
                remote(code.at[here], code.at[there], csend_sem.at[way, k - 1], crecv_sem.at[way, k - 1], to)
            )
        return copies

    def weight_copies():
        return [
            remote(wg_in.at[0], wg.at[:, pl.ds(FF2, FF2)], wsend_sem.at[0], wrecv_sem.at[0], partner),
            remote(wu_in.at[0], wu.at[:, pl.ds(FF2, FF2)], wsend_sem.at[1], wrecv_sem.at[1], partner),
            remote(wd_in.at[0], wd.at[pl.ds(FF2, FF2), :], wsend_sem.at[2], wrecv_sem.at[2], partner),
        ]

    def x_copy(k):
        return remote(t_buf.at[0], t_buf.at[k], xsend_sem.at[k - 1], xrecv_sem.at[k - 1], at(dx=k))

    for way in range(2):
        for copy in z_copies(way, 1):
            copy.start()

    slot = lax.broadcasted_iota(jnp.int32, (CAP, TOK), 0).astype(F32)

    def slot_parts(d):
        for k in range(YN):
            expert = ((y + k) % YN) * ZN + z
            line = code[d, pl.ds(expert, 1), :]
            scale = jnp.floor(line * (1.0 / 64.0))
            yield slot == line - 64.0 * scale, scale * (1.0 / 64.0)

    def y_copies(d):
        j, core = chunk_of(d), owner(d)
        return [
            remote(
                d_buf.at[d, pl.ds(CAP * k, CAP), :],
                r_buf.at[j, pl.ds(CAP * k, CAP), pl.ds(half, HALF)],
                ysend_sem.at[d], yrecv_sem.at[j], at(dy=k, core=core),
            )
            for k in range(1, YN)
        ]

    def y_own_copy(d):
        return remote(
            d_buf.at[d, pl.ds(0, CAP), :],
            r_buf.at[chunk_of(d), pl.ds(0, CAP), pl.ds(half, HALF)],
            ysend0_sem.at[d], yrecv0_sem.at[chunk_of(d)], partner,
        )

    def dispatch(d):
        pick = jnp.concatenate([jnp.where(hit, 1.0, 0.0) for hit, _ in slot_parts(d)], axis=0).astype(BF16)
        for cols in (pl.ds(0, QUARTER), pl.ds(QUARTER, QUARTER)):
            d_buf[d, :, cols] = jnp.dot(pick, g_buf[d, :, cols], preferred_element_type=F32).astype(BF16)
        for copy in y_copies(d):
            copy.start()

        @pl.when(r == owner(d))
        def _():
            r_buf[chunk_of(d), pl.ds(0, CAP), pl.ds(half, HALF)] = d_buf[d, pl.ds(0, CAP), :]

        @pl.when(r != owner(d))
        def _():
            y_own_copy(d).start()

    def z_arrived(k):
        for way in range(2):
            for copy in z_copies(way, k):
                copy.wait_recv()
            if k < ZN // 2:
                for copy in z_copies(way, k + 1):
                    copy.start()

    def experts(j):
        await_bytes(r_buf.at[j, pl.ds(CAP, 3 * CAP), :], yrecv_sem.at[j])
        await_bytes(r_buf.at[j, pl.ds(0, CAP), pl.ds(other, HALF)], yrecv0_sem.at[j])

        def up_step(n, carry):
            cols = pl.ds(pl.multiple_of(n * 256, 256), 256)
            gate_value = jnp.dot(r_buf[j], wg[:, cols], preferred_element_type=F32)
            up_value = jnp.dot(r_buf[j], wu[:, cols], preferred_element_type=F32)
            h_buf[:, cols] = (jax.nn.silu(gate_value) * up_value).astype(BF16)
            return carry

        lax.fori_loop(0, FF // 256, up_step, 0)

        def down_step(n, carry):
            cols = pl.ds(pl.multiple_of(n * 256, 256), 256)
            o_buf[j, :, cols] = jnp.dot(h_buf[...], wd[:, cols], preferred_element_type=F32).astype(BF16)
            return carry

        lax.fori_loop(0, D // 256, down_step, 0)

    def back_copies(j):
        d = jnp.where(r == 0, j, ZN - 1 - j)
        copies = []
        for k in range(1, YN):
            for cols, core in ((half, r), (other, 1 - r)):
                copies.append(
                    remote(
                        o_buf.at[j, pl.ds(CAP * k, CAP), pl.ds(cols, HALF)],
                        q_buf.at[d, pl.ds(CAP * k, CAP), :],
                        bsend_sem.at[j], brecv_sem.at[d], at(dy=-k, core=core),
                    )
                )
        return copies

    def back_own_copy(j):
        d = jnp.where(r == 0, j, ZN - 1 - j)
        return remote(
            o_buf.at[j, pl.ds(0, CAP), pl.ds(other, HALF)], q_buf.at[d, pl.ds(0, CAP), :],
            bsend0_sem.at[j], brecv0_sem.at[d], partner,
        )

    def give_back(j):
        d = jnp.where(r == 0, j, ZN - 1 - j)
        for copy in back_copies(j):
            copy.start()
        back_own_copy(j).start()
        q_buf[d, pl.ds(0, CAP), :] = o_buf[j, pl.ds(0, CAP), pl.ds(half, HALF)]

    def shared_copies():
        copies = []
        for k in range(XN):
            for crel, (cols, core) in enumerate(((half, r), (other, 1 - r))):
                if k or crel:
                    copies.append(
                        remote(
                            sh_buf.at[k, :, pl.ds(cols, HALF)], s_in.at[2 * k + crel - 1],
                            ssend_sem.at[2 * k + crel - 1], srecv_sem.at[0], at(dx=-k, core=core),
                        )
                    )
        return copies

    def shared():
        for k in range(1, XN):
            x_copy(k).wait_recv()
        for k in range(XN):
            gate_value = jnp.dot(t_buf[k], sgu[:, :SF], preferred_element_type=F32)
            up_value = jnp.dot(t_buf[k], sgu[:, SF:], preferred_element_type=F32)
            h_buf[pl.ds(0, TOK), pl.ds(0, SF)] = (jax.nn.silu(gate_value) * up_value).astype(BF16)

            def down_step(n, carry):
                cols = pl.ds(pl.multiple_of(n * 256, 256), 256)
                sh_buf[k, :, cols] = jnp.dot(
                    h_buf[pl.ds(0, TOK), pl.ds(0, SF)], sd[:, cols], preferred_element_type=F32
                ).astype(BF16)
                return carry

            lax.fori_loop(0, D // 256, down_step, 0)
        for copy in shared_copies():
            copy.start()

    def combined(d):
        await_bytes(q_buf.at[d, pl.ds(CAP, 3 * CAP), :], brecv_sem.at[d])

        @pl.when(r != owner(d))
        def _():
            await_bytes(q_buf.at[d, pl.ds(0, CAP), :], brecv0_sem.at[d])

        spread = jnp.concatenate([jnp.where(hit, scale, 0.0) for hit, scale in slot_parts(d)], axis=0).astype(BF16)
        return [
            lax.dot_general(
                spread, q_buf[d, :, pl.ds(part * QUARTER, QUARTER)], (((0,), (0,)), ((), ())),
                preferred_element_type=F32,
            )
            for part in range(2)
        ]

    def r_copy(way, step):
        outgoing, incoming = (plus_out, plus_in) if way == 0 else (minus_out, minus_in)
        if step == 0:
            cols = pl.ds(way * QUARTER, QUARTER)
            src, dst = outgoing.at[0, :, cols], incoming.at[0, :, cols]
        else:
            src, dst = outgoing.at[step], incoming.at[step]
        return remote(
            src, dst, rsend_sem.at[way, step], rrecv_sem.at[way, step], at(dz=1 if way == 0 else -1)
        )

    for copy in weight_copies():
        copy.start()
    dispatch(0)
    for k in range(1, XN):
        x_copy(k).start()
    z_arrived(1)
    dispatch(1)
    dispatch(7)
    for i in range(3):
        pltpu.make_async_copy(loads[i][0], loads[i][1], load_sem.at[i]).wait()
    for copy in weight_copies():
        copy.wait_recv()
    z_arrived(2)
    dispatch(2)
    dispatch(6)
    experts(0)
    z_arrived(3)
    dispatch(3)
    dispatch(5)
    z_arrived(4)
    dispatch(4)
    experts(1)
    for i in range(3, 6):
        pltpu.make_async_copy(loads[i][0], loads[i][1], load_sem.at[i]).wait()
    shared()
    experts(2)
    experts(3)
    for j in (3, 2, 1, 0):
        give_back(j)

    lo, hi = combined(4)
    plus_out[0, :, pl.ds(0, QUARTER)] = lo.astype(BF16)
    r_copy(0, 0).start()
    minus_out[0, :, pl.ds(QUARTER, QUARTER)] = hi.astype(BF16)
    r_copy(1, 0).start()
    for step in range(1, 4):
        for way in range(2):
            d = 4 - step if way == 0 else 4 + step
            outgoing, incoming = (plus_out, plus_in) if way == 0 else (minus_out, minus_in)
            sums = combined(d)
            r_copy(way, step - 1).wait_recv()
            for part in range(2):
                cols = pl.ds(part * QUARTER, QUARTER)
                if step > 1 or part == way:
                    total = sums[part] + incoming[step - 1, :, cols].astype(F32)
                else:
                    total = sums[part]
                outgoing[step, :, cols] = total.astype(BF16)
            r_copy(way, step).start()

    sums = combined(0)
    await_bytes(s_in, srecv_sem.at[0])
    r_copy(0, 3).wait_recv()
    r_copy(1, 3).wait_recv()
    for part in range(2):
        cols = pl.ds(part * QUARTER, QUARTER)
        total = sh_buf[0, :, pl.ds(pl.multiple_of(half + part * QUARTER, 128), QUARTER)].astype(F32)
        for i in range(2 * XN - 1):
            total = total + s_in[i, :, cols].astype(F32)
        total = total + sums[part] + plus_in[3, :, cols].astype(F32) + minus_in[3, :, cols].astype(F32)
        out[:, cols] = total.astype(BF16)

    for copy in weight_copies():
        copy.wait_send()
    for k in range(1, XN):
        x_copy(k).wait_send()
    for way in range(2):
        for k in range(1, ZN // 2 + 1):
            for copy in z_copies(way, k):
                copy.wait_send()
        for step in range(4):
            r_copy(way, step).wait_send()
    for d in range(ZN):
        await_bytes(d_buf.at[d, pl.ds(CAP, 3 * CAP), :], ysend_sem.at[d])

        @pl.when(r != owner(d))
        def _():
            y_own_copy(d).wait_send()

    for j in range(ZN // 2):
        await_bytes(o_buf.at[j, pl.ds(CAP, 3 * CAP), :], bsend_sem.at[j])
        back_own_copy(j).wait_send()
    for copy in shared_copies():
        copy.wait_send()


def on_device(*args):
    tokens, norm_gain, *rest = args
    vmem = pl.BlockSpec(memory_space=pltpu.VMEM)
    hbm = pl.BlockSpec(memory_space=pl.ANY)
    dma = lambda *shape: pltpu.SemaphoreType.DMA(shape)
    half_z = ZN // 2
    return pl.pallas_call(
        kernel,
        out_shape=jax.ShapeDtypeStruct((TOK, HALF), BF16),
        in_specs=[vmem] * 4 + [hbm] * 6,
        out_specs=vmem,
        scratch_shapes=[
            pltpu.VMEM((XN, TOK, D), BF16),
            pltpu.VMEM((ZN, TOK, HALF), BF16),
            pltpu.VMEM((ZN, EXPERTS, TOK), F32),
            pltpu.VMEM((ZN, ROWS, HALF), BF16),
            pltpu.VMEM((half_z, ROWS, D), BF16),
            pltpu.VMEM((ROWS, FF), BF16),
            pltpu.VMEM((half_z, ROWS, D), BF16),
            pltpu.VMEM((ZN, ROWS, HALF), BF16),
            pltpu.VMEM((4, TOK, HALF), BF16),
            pltpu.VMEM((4, TOK, HALF), BF16),
            pltpu.VMEM((4, TOK, HALF), BF16),
            pltpu.VMEM((4, TOK, HALF), BF16),
            pltpu.VMEM((XN, TOK, D), BF16),
            pltpu.VMEM((2 * XN - 1, TOK, HALF), BF16),
            pltpu.VMEM((D, FF), BF16),
            pltpu.VMEM((D, FF), BF16),
            pltpu.VMEM((FF, D), BF16),
            pltpu.VMEM((D, 2 * SF), BF16),
            pltpu.VMEM((SF, D), BF16),
            dma(6), dma(3), dma(3),
            dma(2, 4), dma(2, 4), dma(2, 4), dma(2, 4),
            dma(ZN), dma(half_z), dma(ZN), dma(half_z),
            dma(half_z), dma(ZN), dma(half_z), dma(ZN),
            dma(2, 4), dma(2, 4),
            dma(3), dma(3), dma(2 * XN - 1), dma(1),
        ],
        compiler_params=pltpu.CompilerParams(
            collective_id=0, has_side_effects=True, vmem_limit_bytes=63 * 2**20
        ),
    )(tokens, norm_gain.reshape(1, D), *rest)


def solution(mesh):
    placed = (
        P(("dp", "expert"), None),
        P(),
        P(("dp", "expert"), None),
        P(("dp", "expert"), None),
        P("expert", None, "tensor"),
        P("expert", None, "tensor"),
        P("expert", "tensor", None),
        P(None, ("dp", "tensor")),
        P(None, ("dp", "tensor")),
        P(("dp", "tensor"), None),
    )
    return jax.shard_map(
        on_device,
        mesh=mesh,
        in_specs=placed,
        out_specs=P(("dp", "expert"), "tensor"),
        check_vma=False,
    )
```

time: 322 us -> 125 us (0.39)
  waiting for transfers between devices: 122 us -> 0 us
  Pallas kernels: 0 us -> 118 us
  blocking collectives: 101 us -> 0 us
  matrix products: 36.2 us -> 0 us
  local copies, waits for them, and re-layouts: 23.7 us -> 5.87 us
  between operations: 15.1 us -> 0.01 us
  other arithmetic: 13.5 us -> 0 us
  starting transfers between devices: 10.3 us -> 0 us
    pallas_call x0 -> x1, Pallas kernels: none -> 118 us  [on_device(): pl.pallas_call(kernel, out_shape=jax.ShapeDtypeStruct((TOK, HALF), BF16),...]
    all_to_all x1 -> x0, blocking collectives: 101 us -> none  [on_device(): lax.all_to_all(outgoing, 'expert', split_axis=0, concat_axis=0, tiled=True)]
    all_to_all x1 -> x0, waiting for transfers between devices: 70.2 us -> none  [on_device(): lax.all_to_all(summed, 'expert', split_axis=0, concat_axis=0, tiled=True)]
    dot_general x12 -> x0, matrix products: 36.2 us -> none  [the longest x1 13.5 us: on_device(): jnp.einsum('jecf,efd->jecd', hidden, w_down, preferred_element_type=jnp.f...]
    all_gather x2 -> x0, waiting for transfers between devices: 29.7 us -> none  [the longest x1 21.8 us: on_device(): arrived = lax.all_gather(arrived, 'tensor', axis=2, tiled=True)]
    reduce_scatter x2 -> x0, waiting for transfers between devices: 21.6 us -> none  [the longest x1 21.6 us: on_device(): lax.psum_scatter(partial_out.astype(jnp.bfloat16), 'tensor', scatter_dime...]
    gather x2 -> x0, local copies, waits for them, and re-layouts: 13.8 us -> none  [the longest x1 7.81 us: on_device(): table[position].reshape(tok_rows, TOP, half_width).astype(jnp.float32)]
    all_to_all x1 -> x0, starting transfers between devices: 9.96 us -> none  [on_device(): lax.all_to_all(summed, 'expert', split_axis=0, concat_axis=0, tiled=True)]
  transfers between devices with their start and end apart: 5 -> 0, of which waited for: 4 -> 0; matrix products, arithmetic and copies ran while one was open for 9% -> 0% of each run, Pallas kernels for 0% -> 0%
where the time goes in v1:
time: 125 us; the launch traced here: 124 us
  Pallas kernels  118 us (94%)
  local copies, waits for them, and re-layouts  5.87 us (5%)
    pallas_call x1, Pallas kernels, on_device(): pl.pallas_call(kernel, out_shape=jax.ShapeDtypeStruct((TOK, HALF), BF16),...  118 us
    unnamed x3, local copies, waits for them, and re-layouts  4.56 us

profile of v1, /device:TPU:2, one launch (start us, length us, event | category | flops | bytes accessed | tf_op | source)
XLA Modules:
  0.0 123.9 jit_solution(4891769607526326056)
XLA Ops:
  0.0 1.3 %reshape.3.gain = f32[1,2560]{1,0:T(1,128)} reshape(f32[2560]{0:T(1024)} %param.11) | data formatting | bytes 20480 | tf_op jit(solution)/shard_map/reshape | solution.py:436
  1.3 1.4 %copy.11.ids = s32[128,6]{1,0:T(8,128)} copy(s32[128,6]{0,1:T(8,128)} %param.12) | data formatting | bytes 6144 | tf_op args[2]
  2.7 1.4 %copy.12.weights = s32[128,6]{1,0:T(8,128)} copy(s32[128,6]{0,1:T(8,128)} %param.13) | data formatting | bytes 6144 | tf_op args[3]
  4.2 118.1 %shard_map.100 = bf16[128,1280]{1,0:T(8,128)(2,1)} custom-call(bf16[128,2560]{1,0:T(8,128)(2,1)} %tokens.1, f32[1,2560]{1,0:T(1,128)} %reshape.3.gain, s32[128,6]{1,0:T(8,128)} %copy.11.ids, s32[128,6]{1,0:T(8,128)} %copy.12.weights, bf16[1,2560,384]{2,1,0:T(8,128)(2,1)} %wg_in.1, bf16[1,2560,384]{2,1,0:T(8,128)(2,1)} %wu_in.1, bf16[1,384,2560]{2,1,0:T(8,128)(2,1)} %wd_in.1, ...), custom_call_target="tpu_custom_call" | custom-call | tf_op jit(solution)/shard_map/pallas_call | solution.py:401
  122.2 1.7 %copy.14 = bf16[128,1280]{1,0:T(8,128)(2,1)} copy(bf16[128,1280]{1,0:T(8,128)(2,1)} %shard_map.100) | data formatting | bytes 655360

commit v2 on v1

v2 whole, which is shorter than its diff:
```python
import jax
import jax.numpy as jnp
from jax import lax
from jax.experimental import pallas as pl
from jax.experimental.pallas import tpu as pltpu
from jax.sharding import PartitionSpec as P

D = 2560
HALF = D // 2
QUARTER = HALF // 2
FF2 = 384
FF = 768
SF = 256
EXPERTS = 32
TOP = 6
TOK = 128
CAP = 48
YN = 4
ZN = 8
XN = 4
ROWS = YN * CAP
EPSILON = 1e-06
MESH = pl.DeviceIdType.MESH
BF16 = jnp.bfloat16
F32 = jnp.float32


def owner(d):
    return 0 if d < ZN // 2 else 1


def chunk_of(d):
    return d if d < ZN // 2 else ZN - 1 - d


def kernel(
    tokens, gain, ids, weights, wg_in, wu_in, wd_in, sg_in, su_in, sd_in,
    out,
    t_buf, g_buf, code, d_buf, r_buf, h_buf, o_buf, q_buf,
    plus_in, minus_in, plus_out, minus_out, sh_hidden, sh_buf, s_in,
    wg, wu, wd, sgu, sd,
    load_sem, wsend_sem, wrecv_sem,
    zsend_sem, zrecv_sem, csend_sem, crecv_sem,
    ysend_sem, yrecv_sem, ysend0_sem, yrecv0_sem,
    bsend_sem, brecv_sem, bsend0_sem, brecv0_sem,
    rsend_sem, rrecv_sem,
    xsend_sem, xrecv_sem, ssend_sem, srecv_sem,
):
    x = lax.axis_index("dp")
    e = lax.axis_index("expert")
    r = lax.axis_index("tensor")
    y = e // ZN
    z = e % ZN
    half = pl.multiple_of(r * HALF, 128)
    other = pl.multiple_of((1 - r) * HALF, 128)

    def at(dx=0, dy=0, dz=0, core=None):
        return (
            (x + dx + XN) % XN,
            ((y + dy + YN) % YN) * ZN + (z + dz + ZN) % ZN,
            r if core is None else core,
        )

    partner = at(core=1 - r)

    def remote(src, dst, send, recv, device):
        return pltpu.make_async_remote_copy(
            src_ref=src, dst_ref=dst, send_sem=send, recv_sem=recv,
            device_id=device, device_id_type=MESH,
        )

    def await_bytes(ref, sem):
        pltpu.make_async_copy(ref, ref, sem).wait()

    barrier = pltpu.get_barrier_semaphore()
    peers = [partner, at(dz=1), at(dz=-1)]
    for k in range(1, YN):
        peers += [at(dy=k), at(dy=k, core=1 - r)]
    for k in range(1, XN):
        peers += [at(dx=k), at(dx=k, core=1 - r)]
    for peer in peers:
        pl.semaphore_signal(barrier, inc=1, device_id=peer, device_id_type=MESH)

    loads = [
        (wg_in.at[0], wg.at[:, pl.ds(0, FF2)]),
        (wu_in.at[0], wu.at[:, pl.ds(0, FF2)]),
        (wd_in.at[0], wd.at[pl.ds(0, FF2), :]),
        (sg_in, sgu.at[:, pl.ds(0, SF)]),
        (su_in, sgu.at[:, pl.ds(SF, SF)]),
        (sd_in, sd),
    ]
    for i, (src, dst) in enumerate(loads):
        pltpu.make_async_copy(src, dst, load_sem.at[i]).start()

    gain_row = gain[...].reshape(1, D)

    def norm_step(i, carry):
        rows = pl.ds(pl.multiple_of(i * 16, 16), 16)
        values = tokens[rows, :].astype(F32)
        inverse = lax.rsqrt(jnp.mean(values * values, axis=1, keepdims=True) + EPSILON)
        normed = values * inverse * gain_row
        t_buf[rows, :] = normed.astype(BF16)
        g_buf[0, rows, :] = jnp.where(r == 0, normed[:, :HALF], normed[:, HALF:]).astype(BF16)
        return carry

    lax.fori_loop(0, TOK // 16, norm_step, 0)

    expert_row = lax.broadcasted_iota(jnp.int32, (EXPERTS, TOK), 0)
    named = jnp.zeros((EXPERTS, TOK), F32)
    weight = jnp.zeros((EXPERTS, TOK), F32)
    for k in range(TOP):
        match = ids[k : k + 1, :] == expert_row
        named = jnp.where(match, 1.0, named)
        weight = jnp.where(match, weights[k : k + 1, :].astype(F32), weight)
    before = lax.broadcasted_iota(jnp.int32, (TOK, TOK), 0) < lax.broadcasted_iota(jnp.int32, (TOK, TOK), 1)
    earlier = jnp.where(before, 1.0, 0.0).astype(BF16)
    rank = jnp.dot(named.astype(BF16), earlier, preferred_element_type=F32)
    code[0] = jnp.where(named > 0.5, weight * 64.0 + rank, -1.0)

    pl.semaphore_wait(barrier, len(peers))

    def z_pieces(k):
        return [(way, part) for part in range(2) for way in range(2) if k < ZN // 2 or way == part]

    def z_copies(k, way, part):
        if way == 0:
            here, there, to = k - 1, k, at(dz=-1)
        else:
            here, there, to = (ZN - (k - 1)) % ZN, ZN - k, at(dz=1)
        cols = pl.ds(part * QUARTER, QUARTER)
        copies = [
            remote(
                g_buf.at[here, :, cols], g_buf.at[there, :, cols],
                zsend_sem.at[way, part, k - 1], zrecv_sem.at[way, part, k - 1], to,
            )
        ]
        if part == 0 and (k < ZN // 2 or way == 0):
            copies.append(
                remote(code.at[here], code.at[there], csend_sem.at[way, k - 1], crecv_sem.at[way, k - 1], to)
            )
        return copies

    def weight_copies():
        return [
            remote(wg_in.at[0], wg.at[:, pl.ds(FF2, FF2)], wsend_sem.at[0], wrecv_sem.at[0], partner),
            remote(wu_in.at[0], wu.at[:, pl.ds(FF2, FF2)], wsend_sem.at[1], wrecv_sem.at[1], partner),
            remote(wd_in.at[0], wd.at[pl.ds(FF2, FF2), :], wsend_sem.at[2], wrecv_sem.at[2], partner),
        ]

    def x_copy(k):
        return remote(t_buf.at[pl.ds(0, TOK)], t_buf.at[pl.ds(TOK * k, TOK)], xsend_sem.at[k - 1], xrecv_sem.at[k - 1], at(dx=k))

    for piece in z_pieces(1):
        for copy in z_copies(1, *piece):
            copy.start()

    slot = lax.broadcasted_iota(jnp.int32, (CAP, TOK), 0).astype(F32)

    def slot_parts(d):
        for k in range(YN):
            expert = ((y + k) % YN) * ZN + z
            line = code[d, pl.ds(expert, 1), :]
            scale = jnp.floor(line * (1.0 / 64.0))
            yield slot == line - 64.0 * scale, scale * (1.0 / 64.0)

    def y_copies(d):
        j, core = chunk_of(d), owner(d)
        return [
            remote(
                d_buf.at[d, pl.ds(CAP * k, CAP), :],
                r_buf.at[pl.ds(ROWS * j + CAP * k, CAP), pl.ds(half, HALF)],
                ysend_sem.at[d], yrecv_sem.at[j], at(dy=k, core=core),
            )
            for k in range(1, YN)
        ]

    def y_own_copy(d):
        return remote(
            d_buf.at[d, pl.ds(0, CAP), :],
            r_buf.at[pl.ds(ROWS * chunk_of(d), CAP), pl.ds(half, HALF)],
            ysend0_sem.at[d], yrecv0_sem.at[chunk_of(d)], partner,
        )

    def dispatch(d):
        pick = jnp.concatenate([jnp.where(hit, 1.0, 0.0) for hit, _ in slot_parts(d)], axis=0).astype(BF16)
        for cols in (pl.ds(0, QUARTER), pl.ds(QUARTER, QUARTER)):
            d_buf[d, :, cols] = jnp.dot(pick, g_buf[d, :, cols], preferred_element_type=F32).astype(BF16)
        for copy in y_copies(d):
            copy.start()

        @pl.when(r == owner(d))
        def _():
            r_buf[pl.ds(ROWS * chunk_of(d), CAP), pl.ds(half, HALF)] = d_buf[d, pl.ds(0, CAP), :]

        @pl.when(r != owner(d))
        def _():
            y_own_copy(d).start()

    def z_arrived(k):
        for piece in z_pieces(k):
            for copy in z_copies(k, *piece):
                copy.wait_recv()
            if k < ZN // 2 and piece in z_pieces(k + 1):
                for copy in z_copies(k + 1, *piece):
                    copy.start()

    def experts(*chunks):
        for j in chunks:
            await_bytes(r_buf.at[pl.ds(ROWS * j + CAP, 3 * CAP), :], yrecv_sem.at[j])
            await_bytes(r_buf.at[pl.ds(ROWS * j, CAP), pl.ds(other, HALF)], yrecv0_sem.at[j])
        rows = pl.ds(ROWS * chunks[0], ROWS * len(chunks))
        top = pl.ds(0, ROWS * len(chunks))

        def up_step(n, carry):
            cols = pl.ds(pl.multiple_of(n * 256, 256), 256)
            gate_value = jnp.dot(r_buf[rows, :], wg[:, cols], preferred_element_type=F32)
            up_value = jnp.dot(r_buf[rows, :], wu[:, cols], preferred_element_type=F32)
            h_buf[top, cols] = (jax.nn.silu(gate_value) * up_value).astype(BF16)
            return carry

        lax.fori_loop(0, FF // 256, up_step, 0)

        def down_step(n, carry):
            cols = pl.ds(pl.multiple_of(n * 256, 256), 256)
            o_buf[rows, cols] = jnp.dot(h_buf[top, :], wd[:, cols], preferred_element_type=F32).astype(BF16)
            return carry

        lax.fori_loop(0, D // 256, down_step, 0)

    def back_copies(j):
        d = jnp.where(r == 0, j, ZN - 1 - j)
        copies = []
        for k in range(1, YN):
            for cols, core in ((half, r), (other, 1 - r)):
                copies.append(
                    remote(
                        o_buf.at[pl.ds(ROWS * j + CAP * k, CAP), pl.ds(cols, HALF)],
                        q_buf.at[d, pl.ds(CAP * k, CAP), :],
                        bsend_sem.at[j], brecv_sem.at[d], at(dy=-k, core=core),
                    )
                )
        return copies

    def back_own_copy(j):
        d = jnp.where(r == 0, j, ZN - 1 - j)
        return remote(
            o_buf.at[pl.ds(ROWS * j, CAP), pl.ds(other, HALF)], q_buf.at[d, pl.ds(0, CAP), :],
            bsend0_sem.at[j], brecv0_sem.at[d], partner,
        )

    def give_back(j):
        d = jnp.where(r == 0, j, ZN - 1 - j)
        for copy in back_copies(j):
            copy.start()
        back_own_copy(j).start()
        q_buf[d, pl.ds(0, CAP), :] = o_buf[pl.ds(ROWS * j, CAP), pl.ds(half, HALF)]

    def shared_copies():
        copies = []
        for k in range(XN):
            for crel, (cols, core) in enumerate(((half, r), (other, 1 - r))):
                if k or crel:
                    copies.append(
                        remote(
                            sh_buf.at[pl.ds(TOK * k, TOK), pl.ds(cols, HALF)], s_in.at[2 * k + crel - 1],
                            ssend_sem.at[2 * k + crel - 1], srecv_sem.at[0], at(dx=-k, core=core),
                        )
                    )
        return copies

    def shared():
        for k in range(1, XN):
            x_copy(k).wait_recv()
        gate_value = jnp.dot(t_buf[...], sgu[:, :SF], preferred_element_type=F32)
        up_value = jnp.dot(t_buf[...], sgu[:, SF:], preferred_element_type=F32)
        sh_hidden[...] = (jax.nn.silu(gate_value) * up_value).astype(BF16)

        def down_step(n, carry):
            cols = pl.ds(pl.multiple_of(n * 256, 256), 256)
            sh_buf[:, cols] = jnp.dot(sh_hidden[...], sd[:, cols], preferred_element_type=F32).astype(BF16)
            return carry

        lax.fori_loop(0, D // 256, down_step, 0)
        for copy in shared_copies():
            copy.start()

    def combined(d):
        await_bytes(q_buf.at[d, pl.ds(CAP, 3 * CAP), :], brecv_sem.at[d])

        @pl.when(r != owner(d))
        def _():
            await_bytes(q_buf.at[d, pl.ds(0, CAP), :], brecv0_sem.at[d])

        spread = jnp.concatenate([jnp.where(hit, scale, 0.0) for hit, scale in slot_parts(d)], axis=0).astype(BF16)
        return [
            lax.dot_general(
                spread, q_buf[d, :, pl.ds(part * QUARTER, QUARTER)], (((0,), (0,)), ((), ())),
                preferred_element_type=F32,
            )
            for part in range(2)
        ]

    def r_copy(step, way, part):
        outgoing, incoming = (plus_out, plus_in) if way == 0 else (minus_out, minus_in)
        cols = pl.ds(part * QUARTER, QUARTER)
        return remote(
            outgoing.at[step, :, cols], incoming.at[step, :, cols],
            rsend_sem.at[way, part, step], rrecv_sem.at[way, part, step], at(dz=1 if way == 0 else -1),
        )

    for copy in weight_copies():
        copy.start()
    dispatch(0)
    for k in range(1, XN):
        x_copy(k).start()
    z_arrived(1)
    dispatch(1)
    dispatch(7)
    z_arrived(2)
    dispatch(2)
    dispatch(6)
    z_arrived(3)
    dispatch(3)
    dispatch(5)
    z_arrived(4)
    dispatch(4)
    for i in range(3):
        pltpu.make_async_copy(loads[i][0], loads[i][1], load_sem.at[i]).wait()
    for copy in weight_copies():
        copy.wait_recv()
    experts(0, 1)
    for i in range(3, 6):
        pltpu.make_async_copy(loads[i][0], loads[i][1], load_sem.at[i]).wait()
    shared()
    experts(2)
    give_back(2)
    experts(3)
    give_back(3)
    give_back(1)
    give_back(0)

    sums = combined(4)
    for way in range(2):
        outgoing = plus_out if way == 0 else minus_out
        outgoing[0, :, pl.ds(way * QUARTER, QUARTER)] = sums[way].astype(BF16)
        r_copy(0, way, way).start()
    for step in range(1, 4):
        both = [combined(4 - step), combined(4 + step)]
        for i in range(2):
            for way in range(2):
                part = 1 - i if way == 0 else i
                outgoing, incoming = (plus_out, plus_in) if way == 0 else (minus_out, minus_in)
                cols = pl.ds(part * QUARTER, QUARTER)
                total = both[way][part]
                if step > 1 or part == way:
                    r_copy(step - 1, way, part).wait_recv()
                    total = total + incoming[step - 1, :, cols].astype(F32)
                outgoing[step, :, cols] = total.astype(BF16)
                r_copy(step, way, part).start()

    sums = combined(0)
    await_bytes(s_in, srecv_sem.at[0])
    for part in range(2):
        cols = pl.ds(part * QUARTER, QUARTER)
        total = sh_buf[pl.ds(0, TOK), pl.ds(pl.multiple_of(half + part * QUARTER, 128), QUARTER)].astype(F32)
        for i in range(2 * XN - 1):
            total = total + s_in[i, :, cols].astype(F32)
        both[part] = total + sums[part]
    for way, part in ((0, 1), (1, 0), (0, 0), (1, 1)):
        r_copy(3, way, part).wait_recv()
        incoming = plus_in if way == 0 else minus_in
        both[part] = both[part] + incoming[3, :, pl.ds(part * QUARTER, QUARTER)].astype(F32)
    for part in range(2):
        out[:, pl.ds(part * QUARTER, QUARTER)] = both[part].astype(BF16)

    for copy in weight_copies():
        copy.wait_send()
    for k in range(1, XN):
        x_copy(k).wait_send()
    for k in range(1, ZN // 2 + 1):
        for piece in z_pieces(k):
            for copy in z_copies(k, *piece):
                copy.wait_send()
    for step in range(4):
        for piece in z_pieces(4 - step):
            r_copy(step, *piece).wait_send()
    for d in range(ZN):
        await_bytes(d_buf.at[d, pl.ds(CAP, 3 * CAP), :], ysend_sem.at[d])

        @pl.when(r != owner(d))
        def _():
            y_own_copy(d).wait_send()

    for j in range(ZN // 2):
        await_bytes(o_buf.at[pl.ds(ROWS * j + CAP, 3 * CAP), :], bsend_sem.at[j])
        back_own_copy(j).wait_send()
    for copy in shared_copies():
        copy.wait_send()


def on_device(*args):
    tokens, norm_gain, expert_ids, route_weights, *rest = args
    vmem = pl.BlockSpec(memory_space=pltpu.VMEM)
    hbm = pl.BlockSpec(memory_space=pl.ANY)
    dma = lambda *shape: pltpu.SemaphoreType.DMA(shape)
    half_z = ZN // 2
    return pl.pallas_call(
        kernel,
        out_shape=jax.ShapeDtypeStruct((TOK, HALF), BF16),
        in_specs=[vmem] * 4 + [hbm] * 6,
        out_specs=vmem,
        scratch_shapes=[
            pltpu.VMEM((XN * TOK, D), BF16),
            pltpu.VMEM((ZN, TOK, HALF), BF16),
            pltpu.VMEM((ZN, EXPERTS, TOK), F32),
            pltpu.VMEM((ZN, ROWS, HALF), BF16),
            pltpu.VMEM((half_z * ROWS, D), BF16),
            pltpu.VMEM((2 * ROWS, FF), BF16),
            pltpu.VMEM((half_z * ROWS, D), BF16),
            pltpu.VMEM((ZN, ROWS, HALF), BF16),
            pltpu.VMEM((4, TOK, HALF), BF16),
            pltpu.VMEM((4, TOK, HALF), BF16),
            pltpu.VMEM((4, TOK, HALF), BF16),
            pltpu.VMEM((4, TOK, HALF), BF16),
            pltpu.VMEM((XN * TOK, SF), BF16),
            pltpu.VMEM((XN * TOK, D), BF16),
            pltpu.VMEM((2 * XN - 1, TOK, HALF), BF16),
            pltpu.VMEM((D, FF), BF16),
            pltpu.VMEM((D, FF), BF16),
            pltpu.VMEM((FF, D), BF16),
            pltpu.VMEM((D, 2 * SF), BF16),
            pltpu.VMEM((SF, D), BF16),
            dma(6), dma(3), dma(3),
            dma(2, 2, 4), dma(2, 2, 4), dma(2, 4), dma(2, 4),
            dma(ZN), dma(half_z), dma(ZN), dma(half_z),
            dma(half_z), dma(ZN), dma(half_z), dma(ZN),
            dma(2, 2, 4), dma(2, 2, 4),
            dma(3), dma(3), dma(2 * XN - 1), dma(1),
        ],
        compiler_params=pltpu.CompilerParams(
            collective_id=0, has_side_effects=True, vmem_limit_bytes=63 * 2**20
        ),
    )(tokens, norm_gain, expert_ids.T, route_weights.T, *rest)


def solution(mesh):
    placed = (
        P(("dp", "expert"), None),
        P(),
        P(("dp", "expert"), None),
        P(("dp", "expert"), None),
        P("expert", None, "tensor"),
        P("expert", None, "tensor"),
        P("expert", "tensor", None),
        P(None, ("dp", "tensor")),
        P(None, ("dp", "tensor")),
        P(("dp", "tensor"), None),
    )
    return jax.shard_map(
        on_device,
        mesh=mesh,
        in_specs=placed,
        out_specs=P(("dp", "expert"), "tensor"),
        check_vma=False,
    )
```

time: 125 us -> 112 us (0.90)
  Pallas kernels: 118 us -> 110 us
  local copies, waits for them, and re-layouts: 5.87 us -> 1.72 us
    pallas_call x1, Pallas kernels: 118 us -> 110 us  [on_device(): pl.pallas_call(kernel, out_shape=jax.ShapeDtypeStruct((TOK, HALF), BF16),...]
    unnamed x3 -> x1, local copies, waits for them, and re-layouts: 4.56 us -> 1.72 us
    reshape x1 -> x0, local copies, waits for them, and re-layouts: 1.31 us -> none  [on_device(): norm_gain.reshape(1, D)]
where the time goes in v2:
time: 112 us
  Pallas kernels  110 us (98%)
  local copies, waits for them, and re-layouts  1.72 us (2%)
    pallas_call x1, Pallas kernels, on_device(): pl.pallas_call(kernel, out_shape=jax.ShapeDtypeStruct((TOK, HALF), BF16),...  110 us

profile of v2, /device:TPU:2, one launch (start us, length us, event | category | flops | bytes accessed | tf_op | source)
XLA Modules:
  0.0 111.6 jit_solution(7114057861751485058)
XLA Ops:
  0.0 109.8 %shard_map.100 = bf16[128,1280]{1,0:T(8,128)(2,1)} custom-call(bf16[128,2560]{1,0:T(8,128)(2,1)} %tokens.1, f32[2560]{0:T(1024)} %gain.1, s32[6,128]{1,0:T(8,128)} %bitcast.2, s32[6,128]{1,0:T(8,128)} %bitcast.3, bf16[1,2560,384]{2,1,0:T(8,128)(2,1)} %wg_in.1, bf16[1,2560,384]{2,1,0:T(8,128)(2,1)} %wu_in.1, bf16[1,384,2560]{2,1,0:T(8,128)(2,1)} %wd_in.1, ...), custom_call_target="tpu_custom_call" | custom-call | tf_op jit(solution)/shard_map/pallas_call | solution.py:407
  109.8 1.7 %copy.12 = bf16[128,1280]{1,0:T(8,128)(2,1)} copy(bf16[128,1280]{1,0:T(8,128)(2,1)} %shard_map.100) | data formatting | bytes 655360

commit v3 on v2

v3 whole, which is shorter than its diff:
```python
import jax
import jax.numpy as jnp
from jax import lax
from jax.experimental import pallas as pl
from jax.experimental.pallas import tpu as pltpu
from jax.sharding import PartitionSpec as P

D = 2560
HALF = D // 2
QUARTER = HALF // 2
FF2 = 384
FF = 768
SF = 256
EXPERTS = 32
TOP = 6
TOK = 128
CAP = 48
YN = 4
ZN = 8
XN = 4
ROWS = YN * CAP
EPSILON = 1e-06
MESH = pl.DeviceIdType.MESH
ORDER = (0, 1, 3, 2)
PLACE = {k: CAP * ORDER.index(k) for k in ORDER}
FAR = (0, 7, 1, 4, 6, 2, 5, 3)
NEAR = FAR[:4]
BF16 = jnp.bfloat16
F32 = jnp.float32


def owner(d):
    return 0 if d < ZN // 2 else 1


def signed(d):
    return d if d <= ZN // 2 else d - ZN


def along_y(d):
    return (1, 3) if d in NEAR else (1, 3, 2)


def back_along_y(d):
    return (1, 3) if d in FAR else (1, 3, 2)


def chunk_of(d):
    return d if d < ZN // 2 else ZN - 1 - d


def kernel(
    tokens, gain, ids, weights, wg_in, wu_in, wd_in, sg_in, su_in, sd_in,
    out,
    t_buf, g_buf, code, d_buf, r_buf, h_buf, o_buf, q_buf,
    far_tok, far_code, far_rows, far_q, far_out, far_in,
    plus_in, minus_in, plus_out, minus_out, sh_hidden, sh_buf, s_in,
    wgu, wd, sgu, sd,
    load_sem, wsend_sem, wrecv_sem,
    zsend_sem, zrecv_sem, csend_sem, crecv_sem,
    ysend_sem, yrecv_sem, ysend0_sem, yrecv0_sem,
    bsend_sem, brecv_sem, bsend0_sem, brecv0_sem,
    rsend_sem, rrecv_sem,
    xsend_sem, xrecv_sem, ssend_sem, srecv_sem,
    fsend_sem, frecv_sem, fdsend_sem, fdrecv_sem, fbsend_sem, fbrecv_sem,
):
    x = lax.axis_index("dp")
    e = lax.axis_index("expert")
    r = lax.axis_index("tensor")
    y = e // ZN
    z = e % ZN
    half = pl.multiple_of(r * HALF, 128)
    other = pl.multiple_of((1 - r) * HALF, 128)

    def at(dx=0, dy=0, dz=0, core=None):
        return (
            (x + dx + XN) % XN,
            ((y + dy + YN) % YN) * ZN + (z + dz + ZN) % ZN,
            r if core is None else core,
        )

    partner = at(core=1 - r)
    here_rows = pl.multiple_of(r * (TOK // 2), TOK // 2)
    other_rows = pl.multiple_of((1 - r) * (TOK // 2), TOK // 2)

    def remote(src, dst, send, recv, device):
        return pltpu.make_async_remote_copy(
            src_ref=src, dst_ref=dst, send_sem=send, recv_sem=recv,
            device_id=device, device_id_type=MESH,
        )

    def await_bytes(ref, sem):
        pltpu.make_async_copy(ref, ref, sem).wait()

    barrier = pltpu.get_barrier_semaphore()
    peers = [partner]
    for k in range(1, ZN):
        peers += [at(dz=k), at(dz=k, core=1 - r)]
    for k in range(1, YN):
        peers += [at(dy=k), at(dy=k, core=1 - r)]
    for k in range(1, XN):
        peers += [at(dx=k), at(dx=k, core=1 - r)]
    for peer in peers:
        pl.semaphore_signal(barrier, inc=1, device_id=peer, device_id_type=MESH)

    loads = [
        (wg_in.at[0], wgu.at[:, pl.ds(0, FF2)]),
        (wu_in.at[0], wgu.at[:, pl.ds(FF, FF2)]),
        (wd_in.at[0], wd.at[pl.ds(0, FF2), :]),
        (sg_in, sgu.at[:, pl.ds(0, SF)]),
        (su_in, sgu.at[:, pl.ds(2 * SF, SF)]),
        (sd_in, sd.at[pl.ds(0, SF), :]),
    ]
    for i, (src, dst) in enumerate(loads):
        pltpu.make_async_copy(src, dst, load_sem.at[i]).start()

    gain_row = gain[...].reshape(1, D)

    def norm_step(i, carry):
        rows = pl.ds(pl.multiple_of(i * 16, 16), 16)
        values = tokens[rows, :].astype(F32)
        inverse = lax.rsqrt(jnp.mean(values * values, axis=1, keepdims=True) + EPSILON)
        normed = values * inverse * gain_row
        @pl.when(i // 4 == r)
        def _():
            t_buf[pl.ds(pl.multiple_of((i % 4) * 16, 16), 16), :] = normed.astype(BF16)

        g_buf[0, rows, :] = jnp.where(r == 0, normed[:, :HALF], normed[:, HALF:]).astype(BF16)
        return carry

    lax.fori_loop(0, TOK // 16, norm_step, 0)

    expert_row = lax.broadcasted_iota(jnp.int32, (EXPERTS, TOK), 0)
    named = jnp.zeros((EXPERTS, TOK), F32)
    weight = jnp.zeros((EXPERTS, TOK), F32)
    for k in range(TOP):
        match = ids[k : k + 1, :] == expert_row
        named = jnp.where(match, 1.0, named)
        weight = jnp.where(match, weights[k : k + 1, :].astype(F32), weight)
    before = lax.broadcasted_iota(jnp.int32, (TOK, TOK), 0) < lax.broadcasted_iota(jnp.int32, (TOK, TOK), 1)
    earlier = jnp.where(before, 1.0, 0.0).astype(BF16)
    rank = jnp.dot(named.astype(BF16), earlier, preferred_element_type=F32)
    code[0] = jnp.where(named > 0.5, weight * 64.0 + rank, -1.0)

    pl.semaphore_wait(barrier, len(peers))

    def z_pieces(k):
        return [(way, part) for part in range(2) for way in range(2) if k < ZN // 2 or way == part]

    def z_copies(k, way, part):
        if way == 0:
            here, there, to = k - 1, k, at(dz=-1)
        else:
            here, there, to = (ZN - (k - 1)) % ZN, ZN - k, at(dz=1)
        cols = pl.ds(part * QUARTER, QUARTER)
        copies = [
            remote(
                g_buf.at[here, :, cols], g_buf.at[there, :, cols],
                zsend_sem.at[way, part, k - 1], zrecv_sem.at[way, part, k - 1], to,
            )
        ]
        if part == 0 and (k < ZN // 2 or way == 0):
            copies.append(
                remote(code.at[here], code.at[there], csend_sem.at[way, k - 1], crecv_sem.at[way, k - 1], to)
            )
        return copies

    partner_places = [
        wgu.at[:, pl.ds(FF2, FF2)],
        wgu.at[:, pl.ds(FF + FF2, FF2)],
        wd.at[pl.ds(FF2, FF2), :],
        sgu.at[:, pl.ds(SF, SF)],
        sgu.at[:, pl.ds(3 * SF, SF)],
        sd.at[pl.ds(SF, SF), :],
    ]

    def weight_copy(i):
        return remote(loads[i][0], partner_places[i], wsend_sem.at[i], wrecv_sem.at[i], partner)

    def x_copy(k):
        return remote(t_buf.at[pl.ds(0, TOK // 2)], t_buf.at[pl.ds(TOK // 2 * k, TOK // 2)], xsend_sem.at[k - 1], xrecv_sem.at[k - 1], at(dx=k))

    for piece in z_pieces(1):
        for copy in z_copies(1, *piece):
            copy.start()

    slot = lax.broadcasted_iota(jnp.int32, (CAP, TOK), 0).astype(F32)

    def slot_parts(line_of, experts):
        for expert in experts:
            line = line_of(expert)
            scale = jnp.floor(line * (1.0 / 64.0))
            yield slot == line - 64.0 * scale, scale * (1.0 / 64.0)

    def picks(line_of, experts):
        return jnp.concatenate(
            [jnp.where(hit, 1.0, 0.0) for hit, _ in slot_parts(line_of, experts)], axis=0
        ).astype(BF16)

    def spreads(line_of, experts):
        return jnp.concatenate(
            [jnp.where(hit, scale, 0.0) for hit, scale in slot_parts(line_of, experts)], axis=0
        ).astype(BF16)

    def expert_at(dy=0, dz=0):
        return ((y + dy + YN) % YN) * ZN + (z + dz + ZN) % ZN

    def y_experts(d):
        return [expert_at(dy=k) for k in ORDER if k == 0 or k in along_y(d)]

    def y_copies(d):
        j, core = chunk_of(d), owner(d)
        return [
            remote(
                d_buf.at[d, pl.ds(PLACE[k], CAP), :],
                r_buf.at[pl.ds(ROWS * j + PLACE[k], CAP), pl.ds(half, HALF)],
                ysend_sem.at[d], yrecv_sem.at[j], at(dy=k, core=core),
            )
            for k in along_y(d)
        ]

    def y_own_copy(d):
        return remote(
            d_buf.at[d, pl.ds(0, CAP), :],
            r_buf.at[pl.ds(ROWS * chunk_of(d), CAP), pl.ds(half, HALF)],
            ysend0_sem.at[d], yrecv0_sem.at[chunk_of(d)], partner,
        )

    def dispatch(d):
        pick = picks(lambda expert: code[d, pl.ds(expert, 1), :], y_experts(d))
        rows = pl.ds(0, CAP * (1 + len(along_y(d))))
        for cols in (pl.ds(0, QUARTER), pl.ds(QUARTER, QUARTER)):
            d_buf[d, rows, cols] = jnp.dot(pick, g_buf[d, :, cols], preferred_element_type=F32).astype(BF16)
        for copy in y_copies(d):
            copy.start()

        @pl.when(r == owner(d))
        def _():
            r_buf[pl.ds(ROWS * chunk_of(d), CAP), pl.ds(half, HALF)] = d_buf[d, pl.ds(0, CAP), :]

        @pl.when(r != owner(d))
        def _():
            y_own_copy(d).start()

    def far_copies():
        return [
            remote(g_buf.at[0], far_tok, fsend_sem.at[0], frecv_sem.at[0], at(dy=2)),
            remote(code.at[0], far_code, fsend_sem.at[1], frecv_sem.at[1], at(dy=2)),
        ]

    def far_experts(distances):
        return [expert_at(dz=-signed(d)) for d in distances]

    def far_line(expert):
        return far_code[pl.ds(expert, 1), :]

    def far_row_copy(i):
        d = NEAR[i]
        j = chunk_of(d)
        return remote(
            far_rows.at[pl.ds(CAP * i, CAP), :],
            r_buf.at[pl.ds(ROWS * j + PLACE[2], CAP), pl.ds(half, HALF)],
            fdsend_sem.at[i], fdrecv_sem.at[j],
            partner if d == 0 else at(dz=-signed(d), core=owner(d)),
        )

    def far_pick():
        for copy in far_copies():
            copy.wait_recv()
        pick = picks(far_line, far_experts(NEAR))
        for cols in (pl.ds(0, QUARTER), pl.ds(QUARTER, QUARTER)):
            far_rows[:, cols] = jnp.dot(pick, far_tok[:, cols], preferred_element_type=F32).astype(BF16)

        @pl.when(r == 0)
        def _():
            r_buf[pl.ds(PLACE[2], CAP), pl.ds(half, HALF)] = far_rows[pl.ds(0, CAP), :]

        @pl.when(r == 1)
        def _():
            far_row_copy(0).start()

        for i in (1, 2):
            far_row_copy(i).start()

    def far_pick_two():
        far_row_copy(3).start()

    def z_arrived(k):
        for piece in z_pieces(k):
            for copy in z_copies(k, *piece):
                copy.wait_recv()
            if k < ZN // 2 and piece in z_pieces(k + 1):
                for copy in z_copies(k + 1, *piece):
                    copy.start()

    def experts(j):
        await_bytes(r_buf.at[pl.ds(ROWS * j, CAP), pl.ds(other, HALF)], yrecv0_sem.at[j])
        for core, d in ((0, j), (1, ZN - 1 - j)):

            @pl.when(r == core)
            def _():
                await_bytes(r_buf.at[pl.ds(ROWS * j + CAP, CAP * len(along_y(d))), :], yrecv_sem.at[j])
                if d == 0:
                    await_bytes(r_buf.at[pl.ds(ROWS * j + PLACE[2], CAP), pl.ds(other, HALF)], fdrecv_sem.at[j])
                elif d in NEAR:
                    await_bytes(r_buf.at[pl.ds(ROWS * j + PLACE[2], CAP), :], fdrecv_sem.at[j])

        rows = pl.ds(ROWS * j, ROWS)

        both = jnp.dot(r_buf[rows, :], wgu[...], preferred_element_type=F32)
        h_buf[...] = (jax.nn.silu(both[:, :FF]) * both[:, FF:]).astype(BF16)
        o_buf[rows, :] = jnp.dot(h_buf[...], wd[...], preferred_element_type=F32).astype(BF16)

    def back_copies(j, d):
        copies = []
        for k in back_along_y(d):
            for cols, core in ((half, r), (other, 1 - r)):
                copies.append(
                    remote(
                        o_buf.at[pl.ds(ROWS * j + PLACE[k], CAP), pl.ds(cols, HALF)],
                        q_buf.at[d, pl.ds(PLACE[k], CAP), :],
                        bsend_sem.at[j], brecv_sem.at[d], at(dy=-k, core=core),
                    )
                )
        return copies

    def back_own_copy(j, d):
        return remote(
            o_buf.at[pl.ds(ROWS * j, CAP), pl.ds(other, HALF)], q_buf.at[d, pl.ds(0, CAP), :],
            bsend0_sem.at[j], brecv0_sem.at[d], partner,
        )

    def far_back_copies(j, d):
        i = FAR.index(d)
        copies = []
        for cols, core in ((half, r), (other, 1 - r)):
            if d == 0 and core is r:
                continue
            copies.append(
                remote(
                    o_buf.at[pl.ds(ROWS * j + PLACE[2], CAP), pl.ds(cols, HALF)],
                    far_q.at[pl.ds(CAP * i, CAP), :],
                    fbsend_sem.at[j, 0 if core is r else 1], fbrecv_sem.at[i], at(dz=signed(d), core=core),
                )
            )
        return copies

    def give_back(j, cores=(0, 1)):
        for core in cores:
            d = j if core == 0 else ZN - 1 - j

            @pl.when(r == core)
            def _():
                for copy in back_copies(j, d):
                    copy.start()
                back_own_copy(j, d).start()
                q_buf[d, pl.ds(0, CAP), :] = o_buf[pl.ds(ROWS * j, CAP), pl.ds(half, HALF)]

    def give_far(j):
        for core, d in ((0, j), (1, ZN - 1 - j)):

            @pl.when(r == core)
            def _():
                if d in FAR:
                    for copy in far_back_copies(j, d):
                        copy.start()
                if d == 0:
                    far_q[pl.ds(0, CAP), :] = o_buf[pl.ds(PLACE[2], CAP), pl.ds(half, HALF)]

    def far_out_copy():
        return remote(far_out, far_in, fsend_sem.at[2], frecv_sem.at[2], at(dy=2))

    def far_sum():
        @pl.when(r == 1)
        def _():
            await_bytes(far_q.at[pl.ds(0, CAP), :], fbrecv_sem.at[0])

        for i in range(1, len(FAR)):
            await_bytes(far_q.at[pl.ds(CAP * i, CAP), :], fbrecv_sem.at[i])
        spread = spreads(far_line, far_experts(FAR))
        for cols in (pl.ds(0, QUARTER), pl.ds(QUARTER, QUARTER)):
            far_out[:, cols] = lax.dot_general(
                spread, far_q[:, cols], (((0,), (0,)), ((), ())), preferred_element_type=F32
            ).astype(BF16)
        far_out_copy().start()

    def shared_copies():
        copies = []
        for k in range(1, XN):
            for crel, (cols, core) in enumerate(((half, r), (other, 1 - r))):
                copies.append(
                    remote(
                        sh_buf.at[pl.ds(TOK // 2 * k, TOK // 2), pl.ds(cols, HALF)],
                        s_in.at[k, pl.ds(here_rows, TOK // 2), :],
                        ssend_sem.at[k, crel], srecv_sem.at[0], at(dx=-k, core=core),
                    )
                )
        copies.append(
            remote(
                sh_buf.at[pl.ds(0, TOK // 2), pl.ds(other, HALF)],
                s_in.at[0, pl.ds(here_rows, TOK // 2), :],
                ssend_sem.at[0, 0], srecv_sem.at[1], partner,
            )
        )
        return copies

    def shared():
        for k in range(1, XN):
            x_copy(k).wait_recv()

        both = jnp.dot(t_buf[...], sgu[...], preferred_element_type=F32)
        sh_hidden[...] = (jax.nn.silu(both[:, : 2 * SF]) * both[:, 2 * SF :]).astype(BF16)
        sh_buf[...] = jnp.dot(sh_hidden[...], sd[...], preferred_element_type=F32).astype(BF16)
        for copy in shared_copies():
            copy.start()
        s_in[0, pl.ds(here_rows, TOK // 2), :] = sh_buf[pl.ds(0, TOK // 2), pl.ds(half, HALF)]

    def combined(d):
        await_bytes(q_buf.at[d, pl.ds(CAP, CAP * len(back_along_y(d))), :], brecv_sem.at[d])

        @pl.when(r != owner(d))
        def _():
            await_bytes(q_buf.at[d, pl.ds(0, CAP), :], brecv0_sem.at[d])

        spread = spreads(lambda expert: code[d, pl.ds(expert, 1), :], [expert_at(dy=k) for k in (0,) + back_along_y(d)])
        rows = pl.ds(0, CAP * (1 + len(back_along_y(d))))
        return [
            lax.dot_general(
                spread, q_buf[d, rows, pl.ds(part * QUARTER, QUARTER)], (((0,), (0,)), ((), ())),
                preferred_element_type=F32,
            )
            for part in range(2)
        ]

    def r_copy(step, way, part):
        outgoing, incoming = (plus_out, plus_in) if way == 0 else (minus_out, minus_in)
        cols = pl.ds(part * QUARTER, QUARTER)
        return remote(
            outgoing.at[step, :, cols], incoming.at[step, :, cols],
            rsend_sem.at[way, part, step], rrecv_sem.at[way, part, step], at(dz=1 if way == 0 else -1),
        )

    def loaded(first, last):
        for i in range(first, last):
            pltpu.make_async_copy(loads[i][0], loads[i][1], load_sem.at[i]).wait()
            weight_copy(i).wait_recv()

    dispatch(0)
    for copy in far_copies():
        copy.start()
    z_arrived(1)
    dispatch(1)
    dispatch(7)
    far_pick()
    weight_copy(0).start()
    for k in range(1, XN):
        x_copy(k).start()
    z_arrived(2)
    dispatch(2)
    dispatch(6)
    weight_copy(1).start()
    weight_copy(2).start()
    z_arrived(3)
    dispatch(3)
    dispatch(5)
    far_pick_two()
    loaded(0, 3)
    experts(0)
    give_far(0)
    z_arrived(4)
    dispatch(4)
    for i in range(3, 6):
        weight_copy(i).start()
    experts(1)
    give_far(1)
    experts(2)
    give_far(2)
    give_back(2, (1,))
    experts(3)
    give_far(3)
    give_back(3)
    loaded(3, 6)
    shared()

    sums = combined(4)
    for way in range(2):
        outgoing = plus_out if way == 0 else minus_out
        outgoing[0, :, pl.ds(way * QUARTER, QUARTER)] = sums[way].astype(BF16)
        r_copy(0, way, way).start()
    give_back(2, (0,))
    give_back(1, (1,))
    for step in range(1, 4):
        both = [combined(4 - step), combined(4 + step)]
        for i in range(2):
            for way in range(2):
                part = 1 - i if way == 0 else i
                outgoing, incoming = (plus_out, plus_in) if way == 0 else (minus_out, minus_in)
                cols = pl.ds(part * QUARTER, QUARTER)
                total = both[way][part]
                if step > 1 or part == way:
                    r_copy(step - 1, way, part).wait_recv()
                    total = total + incoming[step - 1, :, cols].astype(F32)
                outgoing[step, :, cols] = total.astype(BF16)
                r_copy(step, way, part).start()
        if step == 1:
            give_back(1, (0,))
            give_back(0)
            far_sum()

    sums = combined(0)
    await_bytes(s_in.at[pl.ds(1, XN - 1)], srecv_sem.at[0])
    await_bytes(s_in.at[0, pl.ds(other_rows, TOK // 2), :], srecv_sem.at[1])
    far_out_copy().wait_recv()
    for part in range(2):
        cols = pl.ds(part * QUARTER, QUARTER)
        total = far_in[:, cols].astype(F32)
        for i in range(XN):
            total = total + s_in[i, :, cols].astype(F32)
        both[part] = total + sums[part]
    for way, part in ((0, 1), (1, 0), (0, 0), (1, 1)):
        r_copy(3, way, part).wait_recv()
        incoming = plus_in if way == 0 else minus_in
        both[part] = both[part] + incoming[3, :, pl.ds(part * QUARTER, QUARTER)].astype(F32)
    for part in range(2):
        out[:, pl.ds(part * QUARTER, QUARTER)] = both[part].astype(BF16)

    for i in range(6):
        weight_copy(i).wait_send()
    for k in range(1, XN):
        x_copy(k).wait_send()
    for k in range(1, ZN // 2 + 1):
        for piece in z_pieces(k):
            for copy in z_copies(k, *piece):
                copy.wait_send()
    for step in range(4):
        for piece in z_pieces(4 - step):
            r_copy(step, *piece).wait_send()
    for d in range(ZN):
        await_bytes(d_buf.at[d, pl.ds(CAP, CAP * len(along_y(d))), :], ysend_sem.at[d])

        @pl.when(r != owner(d))
        def _():
            y_own_copy(d).wait_send()

    for j in range(ZN // 2):
        for core, d in ((0, j), (1, ZN - 1 - j)):

            @pl.when(r == core)
            def _():
                await_bytes(o_buf.at[pl.ds(ROWS * j + CAP, CAP * len(back_along_y(d))), :], bsend_sem.at[j])
                back_own_copy(j, d).wait_send()
                if d in FAR:
                    for copy in far_back_copies(j, d):
                        copy.wait_send()

    for copy in far_copies() + [far_out_copy()]:
        copy.wait_send()
    for i in range(1, len(NEAR)):
        far_row_copy(i).wait_send()

    @pl.when(r == 1)
    def _():
        far_row_copy(0).wait_send()

    for copy in shared_copies():
        copy.wait_send()


def on_device(*args):
    tokens, norm_gain, expert_ids, route_weights, *rest = args
    vmem = pl.BlockSpec(memory_space=pltpu.VMEM)
    hbm = pl.BlockSpec(memory_space=pl.ANY)
    dma = lambda *shape: pltpu.SemaphoreType.DMA(shape)
    half_z = ZN // 2
    return pl.pallas_call(
        kernel,
        out_shape=jax.ShapeDtypeStruct((TOK, HALF), BF16),
        in_specs=[vmem] * 4 + [hbm] * 6,
        out_specs=vmem,
        scratch_shapes=[
            pltpu.VMEM((XN * TOK // 2, D), BF16),
            pltpu.VMEM((ZN, TOK, HALF), BF16),
            pltpu.VMEM((ZN, EXPERTS, TOK), F32),
            pltpu.VMEM((ZN, ROWS, HALF), BF16),
            pltpu.VMEM((half_z * ROWS, D), BF16),
            pltpu.VMEM((ROWS, FF), BF16),
            pltpu.VMEM((half_z * ROWS, D), BF16),
            pltpu.VMEM((ZN, ROWS, HALF), BF16),
            pltpu.VMEM((TOK, HALF), BF16),
            pltpu.VMEM((EXPERTS, TOK), F32),
            pltpu.VMEM((CAP * len(NEAR), HALF), BF16),
            pltpu.VMEM((CAP * len(FAR), HALF), BF16),
            pltpu.VMEM((TOK, HALF), BF16),
            pltpu.VMEM((TOK, HALF), BF16),
            pltpu.VMEM((4, TOK, HALF), BF16),
            pltpu.VMEM((4, TOK, HALF), BF16),
            pltpu.VMEM((4, TOK, HALF), BF16),
            pltpu.VMEM((4, TOK, HALF), BF16),
            pltpu.VMEM((XN * TOK // 2, 2 * SF), BF16),
            pltpu.VMEM((XN * TOK // 2, D), BF16),
            pltpu.VMEM((XN, TOK, HALF), BF16),
            pltpu.VMEM((D, 2 * FF), BF16),
            pltpu.VMEM((FF, D), BF16),
            pltpu.VMEM((D, 4 * SF), BF16),
            pltpu.VMEM((2 * SF, D), BF16),
            dma(6), dma(6), dma(6),
            dma(2, 2, 4), dma(2, 2, 4), dma(2, 4), dma(2, 4),
            dma(ZN), dma(half_z), dma(ZN), dma(half_z),
            dma(half_z), dma(ZN), dma(half_z), dma(ZN),
            dma(2, 2, 4), dma(2, 2, 4),
            dma(3), dma(3), dma(XN, 2), dma(2),
            dma(3), dma(3), dma(5), dma(half_z), dma(half_z, 2), dma(len(FAR)),
        ],
        compiler_params=pltpu.CompilerParams(
            collective_id=0, has_side_effects=True, vmem_limit_bytes=63 * 2**20
        ),
    )(tokens, norm_gain, expert_ids.T, route_weights.T, *rest)


def solution(mesh):
    placed = (
        P(("dp", "expert"), None),
        P(),
        P(("dp", "expert"), None),
        P(("dp", "expert"), None),
        P("expert", None, "tensor"),
        P("expert", None, "tensor"),
        P("expert", "tensor", None),
        P(None, ("dp", "tensor")),
        P(None, ("dp", "tensor")),
        P(("dp", "tensor"), None),
    )
    return jax.shard_map(
        on_device,
        mesh=mesh,
        in_specs=placed,
        out_specs=P(("dp", "expert"), "tensor"),
        check_vma=False,
    )
```

time: 112 us -> 101 us (0.902)
  Pallas kernels: 110 us -> 98.6 us
    pallas_call x1, Pallas kernels: 110 us -> 98.6 us  [on_device(): pl.pallas_call(kernel, out_shape=jax.ShapeDtypeStruct((TOK, HALF), BF16),...]
where the time goes in v3:
time: 101 us; the launch traced here: 100 us
  Pallas kernels  98.6 us (98%)
  local copies, waits for them, and re-layouts  1.72 us (2%)
    pallas_call x1, Pallas kernels, on_device(): pl.pallas_call(kernel, out_shape=jax.ShapeDtypeStruct((TOK, HALF), BF16),...  98.6 us

profile of v3, /device:TPU:2, one launch (start us, length us, event | category | flops | bytes accessed | tf_op | source)
XLA Modules:
  0.0 100.4 jit_solution(2181225904235033284)
XLA Ops:
  0.0 98.6 %shard_map.100 = bf16[128,1280]{1,0:T(8,128)(2,1)} custom-call(bf16[128,2560]{1,0:T(8,128)(2,1)} %tokens.1, f32[2560]{0:T(1024)} %gain.1, s32[6,128]{1,0:T(8,128)} %bitcast.2, s32[6,128]{1,0:T(8,128)} %bitcast.3, bf16[1,2560,384]{2,1,0:T(8,128)(2,1)} %wg_in.1, bf16[1,2560,384]{2,1,0:T(8,128)(2,1)} %wu_in.1, bf16[1,384,2560]{2,1,0:T(8,128)(2,1)} %wd_in.1, ...), custom_call_target="tpu_custom_call" | custom-call | tf_op jit(solution)/shard_map/pallas_call | solution.py:575
  98.6 1.7 %copy.12 = bf16[128,1280]{1,0:T(8,128)(2,1)} copy(bf16[128,1280]{1,0:T(8,128)(2,1)} %shard_map.100) | data formatting | bytes 655360

commit v4 on v3

--- a/solution.py
+++ b/solution.py
@@ -23,8 +23,8 @@
 MESH = pl.DeviceIdType.MESH
 ORDER = (0, 1, 3, 2)
 PLACE = {k: CAP * ORDER.index(k) for k in ORDER}
-FAR = (0, 7, 1, 4, 6, 2, 5, 3)
-NEAR = FAR[:4]
+FAR = (0, 7, 1, 6, 2, 5, 3)
+NEAR = (0, 7, 1, 6, 2)
 BF16 = jnp.bfloat16
 F32 = jnp.float32
 
@@ -94,7 +94,7 @@
 
     barrier = pltpu.get_barrier_semaphore()
     peers = [partner]
-    for k in range(1, ZN):
+    for k in sorted({signed(d) for d in FAR} - {0}):
         peers += [at(dz=k), at(dz=k, core=1 - r)]
     for k in range(1, YN):
         peers += [at(dy=k), at(dy=k, core=1 - r)]
@@ -283,7 +283,8 @@
             far_row_copy(i).start()
 
     def far_pick_two():
-        far_row_copy(3).start()
+        for i in range(3, len(NEAR)):
+            far_row_copy(i).start()
 
     def z_arrived(k):
         for piece in z_pieces(k):
@@ -293,20 +294,20 @@
                 for copy in z_copies(k + 1, *piece):
                     copy.start()
 
-    def experts(j):
-        await_bytes(r_buf.at[pl.ds(ROWS * j, CAP), pl.ds(other, HALF)], yrecv0_sem.at[j])
-        for core, d in ((0, j), (1, ZN - 1 - j)):
+    def experts(*chunks):
+        for core, j in enumerate(chunks):
+            d = j if core == 0 else ZN - 1 - j
 
             @pl.when(r == core)
             def _():
+                await_bytes(r_buf.at[pl.ds(ROWS * j, CAP), pl.ds(other, HALF)], yrecv0_sem.at[j])
                 await_bytes(r_buf.at[pl.ds(ROWS * j + CAP, CAP * len(along_y(d))), :], yrecv_sem.at[j])
                 if d == 0:
                     await_bytes(r_buf.at[pl.ds(ROWS * j + PLACE[2], CAP), pl.ds(other, HALF)], fdrecv_sem.at[j])
                 elif d in NEAR:
                     await_bytes(r_buf.at[pl.ds(ROWS * j + PLACE[2], CAP), :], fdrecv_sem.at[j])
 
-        rows = pl.ds(ROWS * j, ROWS)
-
+        rows = pl.ds(pl.multiple_of(ROWS * jnp.where(r == 0, chunks[0], chunks[1]), 16), ROWS)
         both = jnp.dot(r_buf[rows, :], wgu[...], preferred_element_type=F32)
         h_buf[...] = (jax.nn.silu(both[:, :FF]) * both[:, FF:]).astype(BF16)
         o_buf[rows, :] = jnp.dot(h_buf[...], wd[...], preferred_element_type=F32).astype(BF16)
@@ -345,8 +346,10 @@
             )
         return copies
 
-    def give_back(j, cores=(0, 1)):
-        for core in cores:
+    def give_back(*chunks):
+        for core, j in enumerate(chunks):
+            if j is None:
+                continue
             d = j if core == 0 else ZN - 1 - j
 
             @pl.when(r == core)
@@ -356,8 +359,9 @@
                 back_own_copy(j, d).start()
                 q_buf[d, pl.ds(0, CAP), :] = o_buf[pl.ds(ROWS * j, CAP), pl.ds(half, HALF)]
 
-    def give_far(j):
-        for core, d in ((0, j), (1, ZN - 1 - j)):
+    def give_far(*chunks):
+        for core, j in enumerate(chunks):
+            d = j if core == 0 else ZN - 1 - j
 
             @pl.when(r == core)
             def _():
@@ -451,7 +455,6 @@
     z_arrived(1)
     dispatch(1)
     dispatch(7)
-    far_pick()
     weight_copy(0).start()
     for k in range(1, XN):
         x_copy(k).start()
@@ -461,24 +464,26 @@
     weight_copy(1).start()
     weight_copy(2).start()
     z_arrived(3)
+    dispatch(5)
     dispatch(3)
-    dispatch(5)
-    far_pick_two()
     loaded(0, 3)
-    experts(0)
-    give_far(0)
     z_arrived(4)
     dispatch(4)
+    far_pick()
+    far_pick_two()
     for i in range(3, 6):
         weight_copy(i).start()
-    experts(1)
-    give_far(1)
-    experts(2)
-    give_far(2)
-    give_back(2, (1,))
-    experts(3)
-    give_far(3)
-    give_back(3)
+    experts(0, 0)
+    give_far(0, 0)
+    experts(1, 2)
+    give_far(1, 2)
+    give_back(None, 2)
+    experts(3, 3)
+    give_far(3, 3)
+    give_back(3, 3)
+    experts(2, 1)
+    give_far(2, 1)
+    give_back(2, 1)
     loaded(3, 6)
     shared()
 
@@ -487,8 +492,6 @@
         outgoing = plus_out if way == 0 else minus_out
         outgoing[0, :, pl.ds(way * QUARTER, QUARTER)] = sums[way].astype(BF16)
         r_copy(0, way, way).start()
-    give_back(2, (0,))
-    give_back(1, (1,))
     for step in range(1, 4):
         both = [combined(4 - step), combined(4 + step)]
         for i in range(2):
@@ -503,8 +506,8 @@
                 outgoing[step, :, cols] = total.astype(BF16)
                 r_copy(step, way, part).start()
         if step == 1:
-            give_back(1, (0,))
-            give_back(0)
+            give_back(1, 0)
+            give_back(0, None)
             far_sum()
 
     sums = combined(0)
@@ -609,7 +612,7 @@
             dma(half_z), dma(ZN), dma(half_z), dma(ZN),
             dma(2, 2, 4), dma(2, 2, 4),
             dma(3), dma(3), dma(XN, 2), dma(2),
-            dma(3), dma(3), dma(5), dma(half_z), dma(half_z, 2), dma(len(FAR)),
+            dma(3), dma(3), dma(len(NEAR)), dma(half_z), dma(half_z, 2), dma(len(FAR)),
         ],
         compiler_params=pltpu.CompilerParams(
             collective_id=0, has_side_effects=True, vmem_limit_bytes=63 * 2**20

time: 101 us -> 97.3 us (0.963)
  Pallas kernels: 98.6 us -> 95.3 us
    pallas_call x1, Pallas kernels: 98.6 us -> 95.3 us  [on_device(): pl.pallas_call(kernel, out_shape=jax.ShapeDtypeStruct((TOK, HALF), BF16),...]
where the time goes in v4:
time: 97.3 us; the launch traced here: 97 us
  Pallas kernels  95.3 us (98%)
  local copies, waits for them, and re-layouts  1.72 us (2%)
    pallas_call x1, Pallas kernels, on_device(): pl.pallas_call(kernel, out_shape=jax.ShapeDtypeStruct((TOK, HALF), BF16),...  95.3 us

profile of v4, /device:TPU:2, one launch (start us, length us, event | category | flops | bytes accessed | tf_op | source)
XLA Modules:
  0.0 97.0 jit_solution(14573937877382829785)
XLA Ops:
  0.0 95.3 %shard_map.100 = bf16[128,1280]{1,0:T(8,128)(2,1)} custom-call(bf16[128,2560]{1,0:T(8,128)(2,1)} %tokens.1, f32[2560]{0:T(1024)} %gain.1, s32[6,128]{1,0:T(8,128)} %bitcast.2, s32[6,128]{1,0:T(8,128)} %bitcast.3, bf16[1,2560,384]{2,1,0:T(8,128)(2,1)} %wg_in.1, bf16[1,2560,384]{2,1,0:T(8,128)(2,1)} %wu_in.1, bf16[1,384,2560]{2,1,0:T(8,128)(2,1)} %wd_in.1, ...), custom_call_target="tpu_custom_call" | custom-call | tf_op jit(solution)/shard_map/pallas_call | solution.py:578
  95.3 1.7 %copy.12 = bf16[128,1280]{1,0:T(8,128)(2,1)} copy(bf16[128,1280]{1,0:T(8,128)(2,1)} %shard_map.100) | data formatting | bytes 655360

commit v5 on v4

--- a/solution.py
+++ b/solution.py
@@ -208,39 +208,38 @@
     def y_experts(d):
         return [expert_at(dy=k) for k in ORDER if k == 0 or k in along_y(d)]
 
-    def y_copies(d):
+    def y_copies(d, part):
         j, core = chunk_of(d), owner(d)
+        here = pl.ds(part * QUARTER, QUARTER)
+        there = pl.ds(pl.multiple_of(half + part * QUARTER, 128), QUARTER)
         return [
             remote(
-                d_buf.at[d, pl.ds(PLACE[k], CAP), :],
-                r_buf.at[pl.ds(ROWS * j + PLACE[k], CAP), pl.ds(half, HALF)],
+                d_buf.at[d, pl.ds(PLACE[k], CAP), here],
+                r_buf.at[pl.ds(ROWS * j + PLACE[k], CAP), there],
                 ysend_sem.at[d], yrecv_sem.at[j], at(dy=k, core=core),
             )
             for k in along_y(d)
         ]
 
-    def y_own_copy(d):
-        return remote(
-            d_buf.at[d, pl.ds(0, CAP), :],
-            r_buf.at[pl.ds(ROWS * chunk_of(d), CAP), pl.ds(half, HALF)],
-            ysend0_sem.at[d], yrecv0_sem.at[chunk_of(d)], partner,
-        )
-
-    def dispatch(d):
+    def dispatch(d, parts=(0, 1)):
         pick = picks(lambda expert: code[d, pl.ds(expert, 1), :], y_experts(d))
         rows = pl.ds(0, CAP * (1 + len(along_y(d))))
-        for cols in (pl.ds(0, QUARTER), pl.ds(QUARTER, QUARTER)):
-            d_buf[d, rows, cols] = jnp.dot(pick, g_buf[d, :, cols], preferred_element_type=F32).astype(BF16)
-        for copy in y_copies(d):
-            copy.start()
-
-        @pl.when(r == owner(d))
-        def _():
-            r_buf[pl.ds(ROWS * chunk_of(d), CAP), pl.ds(half, HALF)] = d_buf[d, pl.ds(0, CAP), :]
-
-        @pl.when(r != owner(d))
-        def _():
-            y_own_copy(d).start()
+        for part in parts:
+            here = pl.ds(part * QUARTER, QUARTER)
+            there = pl.ds(pl.multiple_of(half + part * QUARTER, 128), QUARTER)
+            d_buf[d, rows, here] = jnp.dot(pick, g_buf[d, :, here], preferred_element_type=F32).astype(BF16)
+            for copy in y_copies(d, part):
+                copy.start()
+            own = d_buf.at[d, pl.ds(0, CAP), here]
+            own_place = r_buf.at[pl.ds(ROWS * chunk_of(d), CAP), there]
+
+            @pl.when(r == owner(d))
+            def _():
+                own_place[...] = own[...]
+
+            @pl.when(r != owner(d))
+            def _():
+                remote(own, own_place, ysend0_sem.at[d], yrecv0_sem.at[chunk_of(d)], partner).start()
 
     def far_copies():
         return [
@@ -287,12 +286,16 @@
             far_row_copy(i).start()
 
     def z_arrived(k):
-        for piece in z_pieces(k):
-            for copy in z_copies(k, *piece):
+        pieces = z_pieces(k)
+        if k == 3:
+            pieces.sort(key=lambda piece: (piece[1], -piece[0]))
+        for way, part in pieces:
+            for copy in z_copies(k, way, part):
                 copy.wait_recv()
-            if k < ZN // 2 and piece in z_pieces(k + 1):
-                for copy in z_copies(k + 1, *piece):
+            if k < ZN // 2 and (way, part) in z_pieces(k + 1):
+                for copy in z_copies(k + 1, way, part):
                     copy.start()
+            dispatch(k if way == 0 or k == ZN // 2 else ZN - k, (part,))
 
     def experts(*chunks):
         for core, j in enumerate(chunks):
@@ -453,22 +456,15 @@
     for copy in far_copies():
         copy.start()
     z_arrived(1)
-    dispatch(1)
-    dispatch(7)
     weight_copy(0).start()
     for k in range(1, XN):
         x_copy(k).start()
     z_arrived(2)
-    dispatch(2)
-    dispatch(6)
     weight_copy(1).start()
     weight_copy(2).start()
     z_arrived(3)
-    dispatch(5)
-    dispatch(3)
     loaded(0, 3)
     z_arrived(4)
-    dispatch(4)
     far_pick()
     far_pick_two()
     for i in range(3, 6):
@@ -483,7 +479,6 @@
     give_back(3, 3)
     experts(2, 1)
     give_far(2, 1)
-    give_back(2, 1)
     loaded(3, 6)
     shared()
 
@@ -492,6 +487,7 @@
         outgoing = plus_out if way == 0 else minus_out
         outgoing[0, :, pl.ds(way * QUARTER, QUARTER)] = sums[way].astype(BF16)
         r_copy(0, way, way).start()
+    give_back(2, 1)
     for step in range(1, 4):
         both = [combined(4 - step), combined(4 + step)]
         for i in range(2):
@@ -505,8 +501,9 @@
                     total = total + incoming[step - 1, :, cols].astype(F32)
                 outgoing[step, :, cols] = total.astype(BF16)
                 r_copy(step, way, part).start()
+            if step == 1 and i == 0:
+                give_back(1, 0)
         if step == 1:
-            give_back(1, 0)
             give_back(0, None)
             far_sum()
 
@@ -543,7 +540,7 @@
 
         @pl.when(r != owner(d))
         def _():
-            y_own_copy(d).wait_send()
+            await_bytes(d_buf.at[d, pl.ds(0, CAP), :], ysend0_sem.at[d])
 
     for j in range(ZN // 2):
         for core, d in ((0, j), (1, ZN - 1 - j)):

time: 97.3 us -> 95.2 us (0.978)
  Pallas kernels: 95.3 us -> 92.8 us
    pallas_call x1, Pallas kernels: 95.3 us -> 92.8 us  [on_device(): pl.pallas_call(kernel, out_shape=jax.ShapeDtypeStruct((TOK, HALF), BF16),...]
where the time goes in v5:
time: 95.2 us; the launch traced here: 94.6 us
  Pallas kernels  92.8 us (97%)
  local copies, waits for them, and re-layouts  1.72 us (2%)
    pallas_call x1, Pallas kernels, on_device(): pl.pallas_call(kernel, out_shape=jax.ShapeDtypeStruct((TOK, HALF), BF16),...  92.8 us

profile of v5, /device:TPU:2, one launch (start us, length us, event | category | flops | bytes accessed | tf_op | source)
XLA Modules:
  0.0 94.6 jit_solution(6878825122186205020)
XLA Ops:
  0.0 92.8 %shard_map.100 = bf16[128,1280]{1,0:T(8,128)(2,1)} custom-call(bf16[128,2560]{1,0:T(8,128)(2,1)} %tokens.1, f32[2560]{0:T(1024)} %gain.1, s32[6,128]{1,0:T(8,128)} %bitcast.2, s32[6,128]{1,0:T(8,128)} %bitcast.3, bf16[1,2560,384]{2,1,0:T(8,128)(2,1)} %wg_in.1, bf16[1,2560,384]{2,1,0:T(8,128)(2,1)} %wu_in.1, bf16[1,384,2560]{2,1,0:T(8,128)(2,1)} %wd_in.1, ...), custom_call_target="tpu_custom_call" | custom-call | tf_op jit(solution)/shard_map/pallas_call | solution.py:575
  92.9 1.7 %copy.12 = bf16[128,1280]{1,0:T(8,128)(2,1)} copy(bf16[128,1280]{1,0:T(8,128)(2,1)} %shard_map.100) | data formatting | bytes 655360
